TPU v7x, 16 devices: a 4x2x1 block of a 4x4x8 slice. The times are simulated.
16 devices in a mesh: dp: 2 (over y, z), tp: 8 (over x, core).
Axes of the slice: x: 4, y: 2, z: 1, core: 2. Of those that a mesh axis runs over, the one named last changes fastest.
The devices are a block of a 4x4x8 slice.
Arguments:
- x: bfloat16 [8192, 2048], P(('dp', 'tp')), parts along dimension 0
- dy: bfloat16 [8192, 2048], P(('dp', 'tp')), parts along dimension 0
- gate: bfloat16 [8192, 5120], P('dp', 'tp'), parts along dimension 0
- up: bfloat16 [8192, 5120], P('dp', 'tp'), parts along dimension 0
- w_gate: bfloat16 [2048, 5120], P(None, 'tp')
- w_up: bfloat16 [2048, 5120], P(None, 'tp')
- w_down: bfloat16 [5120, 2048], P('tp')
Outputs:
- output 1: bfloat16 [8192, 2048], P(('dp', 'tp')), parts along dimension 0
- output 2: bfloat16 [4096, 5120], P('dp', 'tp'), parts along dimension 0
- output 3: bfloat16 [4096, 5120], P('dp', 'tp'), parts along dimension 0
- output 4: bfloat16 [10240, 2048], P(('dp', 'tp')), parts along dimension 0
There are 2 independent parts. A program takes and returns all parts, laid end to end along the dimension named above; an argument that names none is the same for every part.
All inputs are finite; a program needn't handle non-finite values.
Results may differ from a plain program's by a relative error of at most 0.012.
Values are sent between devices in bfloat16 or wider.
A program may use at most 768 MiB of HBM per device.

v0:
```python
import jax
import jax.numpy as jnp


def act(gate, up):
    return jax.nn.gelu(gate) * up


def solution(mesh):
    def step(x, dy, gate, up, w_gate, w_up, w_down):
        hidden, back = jax.vjp(act, gate.astype(jnp.float32), up.astype(jnp.float32))
        d_hidden = jnp.dot(dy, w_down.T, preferred_element_type=jnp.float32)
        d_gate, d_up = (g.astype(jnp.bfloat16) for g in back(d_hidden))
        dx = jnp.dot(d_gate, w_gate.T) + jnp.dot(d_up, w_up.T)
        groups = mesh.shape["dp"]

        def by_group(a, b):
            a, b = (t.reshape(groups, -1, t.shape[-1]) for t in (a, b))
            product = jnp.einsum("gta,gtb->gab", a, b, preferred_element_type=jnp.float32)
            return product.astype(jnp.bfloat16).reshape(-1, b.shape[-1])

        return dx, by_group(x, d_gate), by_group(x, d_up), by_group(hidden.astype(jnp.bfloat16), dy)

    return step
```

profile of v0, /device:TPU:112, one launch (start us, length us, event | category | flops | bytes accessed | tf_op | source)
XLA Modules:
  0.0 274.7 jit_solution(15790665633530970791)
XLA Ops:
  7.2 0.0 copy-start
  7.2 0.1 all-gather.11.cloned.1.call-start
  7.3 0.7 all-gather.11.cloned.1.call-update
  8.0 0.1 all-gather.13.cloned.1.call-start
  8.1 0.7 all-gather.13.cloned.1.call-update
  8.8 0.1 reduce-scatter.4.cloned.1.call-start
  8.9 84.7 %all-gather.11.cloned.1.call-done = bf16[4096,2048]{1,0:T(8,128)(2,1)} async-done(((bf16[512,2048]{1,0:T(8,128)(2,1)}), bf16[4096,2048]{1,0:T(8,128)(2,1)}) %all-gather.11.cloned.1.call-update) | async-done | bytes 16777232 | tf_op args[1]
  93.6 29.2 %fusion.4 = (bf16[4096,640]{1,0:T(8,128)(2,1)}, f32[4096,640]{1,0:T(8,128)}) fusion(bf16[4096,640]{1,0:T(8,128)(2,1)} %param.3, bf16[4096,640]{1,0:T(8,128)(2,1)} %param.2, bf16[4096,2048]{1,0:T(8,128)(2,1)} %all-gather.11.cloned.1.call-done, bf16[640,2048]{1,0:T(8,128)(2,1)} %param.1), kind=kOutput, calls=%fused_computation.12 | convolution fusion | flops 10797711360 | bytes 45613056 | tf_op jit(solution)/dot_general | solution.py:12
  122.9 0.0 copy-done
  122.9 18.7 %fusion.25 = bf16[4096,2048]{1,0:T(8,128)(2,1)} fusion(bf16[4096,640]{1,0:T(8,128)(2,1)} %get-tuple-element.4, bf16[2048,640]{1,0:T(8,128)(2,1)S(1)} %copy-done), kind=kOutput, calls=%fused_computation.33 | convolution fusion | flops 10737418240 | bytes 24641536 | tf_op jit(solution)/dot_general | solution.py:14
  141.5 23.9 %convolution_add_fusion = bf16[4096,2048]{1,0:T(8,128)(2,1)} fusion(bf16[4096,2048]{1,0:T(8,128)(2,1)} %fusion.25, bf16[2048,640]{1,0:T(8,128)(2,1)} %param.5, f32[4096,640]{1,0:T(8,128)} %get-tuple-element.5, bf16[4096,640]{1,0:T(8,128)(2,1)} %param.3), kind=kOutput, calls=%fused_computation.8 | convolution fusion | flops 10774642688 | bytes 51904512 | tf_op jit(solution)/dot_general | solution.py:14
  165.4 0.1 reduce-scatter.4.cloned.1.call-update
  165.5 11.4 %all-gather.13.cloned.1.call-done = bf16[4096,2048]{1,0:T(8,128)(2,1)} async-done(((bf16[512,2048]{1,0:T(8,128)(2,1)}), bf16[4096,2048]{1,0:T(8,128)(2,1)}) %all-gather.13.cloned.1.call-update) | async-done | bytes 16777232 | tf_op jit(solution)/reshape | solution.py:18
  176.9 21.5 %fusion.20 = bf16[2048,640]{0,1:T(8,128)(2,1)S(1)} fusion(bf16[4096,2048]{1,0:T(8,128)(2,1)} %all-gather.13.cloned.1.call-done, f32[4096,640]{1,0:T(8,128)} %get-tuple-element.5, bf16[4096,640]{1,0:T(8,128)(2,1)} %param.3), kind=kOutput, calls=%fused_computation.28 | convolution fusion | flops 10767564800 | bytes 35127296 | tf_op jit(solution)/gta,gtb->gab/dot_general | solution.py:19
  198.4 2.6 copy.1
  201.0 16.2 %fusion.19 = bf16[2048,640]{0,1:T(8,128)(2,1)S(1)} fusion(bf16[4096,640]{1,0:T(8,128)(2,1)} %get-tuple-element.4, bf16[4096,2048]{1,0:T(8,128)(2,1)} %all-gather.13.cloned.1.call-done), kind=kOutput, calls=%fused_computation.27 | convolution fusion | flops 10738728960 | bytes 24641536 | tf_op jit(solution)/gta,gtb->gab/dot_general | solution.py:19
  217.1 2.6 copy
  219.7 0.0 copy-start.1
  219.7 22.1 %fusion.16 = bf16[640,2048]{1,0:T(8,128)(2,1)} fusion(bf16[4096,2048]{1,0:T(8,128)(2,1)} %all-gather.11.cloned.1.call-done, bf16[4096,640]{1,0:T(8,128)(2,1)} %param.2, bf16[4096,640]{1,0:T(8,128)(2,1)} %param.3), kind=kOutput, calls=%fused_computation.24 | convolution fusion | flops 10770186240 | bytes 29884416 | tf_op jit(solution)/gta,gtb->gab/dot_general | solution.py:19
  241.8 26.3 %reduce-scatter.4.cloned.1.call-done = bf16[512,2048]{1,0:T(8,128)(2,1)} async-done(((bf16[4096,2048]{1,0:T(8,128)(2,1)}), bf16[512,2048]{1,0:T(8,128)(2,1)}) %reduce-scatter.4.cloned.1.call-update) | async-done | bytes 2097168
  268.1 0.0 copy-done.1
Async XLA Ops:
  7.2 115.7 %copy-start = (bf16[2048,640]{1,0:T(8,128)(2,1)S(1)}, bf16[2048,640]{1,0:T(8,128)(2,1)}, u32[]{:S(2)}) copy-start(bf16[2048,640]{1,0:T(8,128)(2,1)} %param.4) | copy-start | bytes 7864324
  7.2 86.4 %all-gather.11.cloned.1.call-start = ((), (), s32[]{:S(2)}) async-start(), calls=%async_computation.1 | async-start | bytes 18874368 | tf_op args[1]
  8.0 168.9 %all-gather.13.cloned.1.call-start = ((), (), s32[]{:S(2)}) async-start(), calls=%async_computation.2 | async-start | bytes 18874368 | tf_op jit(solution)/reshape | solution.py:18
  8.8 259.3 %reduce-scatter.4.cloned.1.call-start = ((), (), s32[]{:S(2)}) async-start(), calls=%async_computation.3 | async-start | bytes 18874368
  219.7 48.4 %copy-start.1 = (bf16[2048,640]{1,0:T(8,128)(2,1)S(1)}, bf16[2048,640]{1,0:T(8,128)(2,1)}, u32[]{:S(2)}) copy-start(bf16[2048,640]{1,0:T(8,128)(2,1)} %param.4) | copy-start | bytes 7864324
Sparse Core Ops, SparseCore 0:
  9.6 83.9 all-gather.10
  95.2 81.6 all-gather.12
  179.8 88.2 reduce-scatter.3
where the time goes:
time: 275 us
  matrix products  132 us (48%)
  waiting for transfers between devices  124 us (45%)
  between operations  13.8 us (5%)
  local copies, waits for them, and re-layouts  5.16 us (2%)
    unnamed x5, waiting for transfers between devices  113 us
    dot_general x3, matrix products, by_group(): jnp.einsum('gta,gtb->gab', a, b, preferred_element_type=jnp.float32)  59.8 us
    dot_general x2, matrix products, step(): dx = jnp.dot(d_gate, w_gate.T) + jnp.dot(d_up, w_up.T)  42.5 us
    dot_general x1, matrix products, step(): d_hidden = jnp.dot(dy, w_down.T, preferred_element_type=jnp.float32)  29.2 us
    reshape x1, waiting for transfers between devices, by_group(): a, b = (t.reshape(groups, -1, t.shape[-1]) for t in (a, b))  11.4 us
  transfers between devices with their start and end apart: 3, of which 3 were waited for; matrix products, arithmetic and copies ran while one was open for 50% of the time, Pallas kernels for 0%

commit v1 on v0

v1 whole, which is shorter than its diff:
```python
import functools

import jax
import jax.numpy as jnp
from jax import lax
from jax.experimental import pallas as pl
from jax.experimental.pallas import tpu as pltpu
from jax.sharding import PartitionSpec as P

MESH = pl.DeviceIdType.MESH
BF16, F32 = jnp.bfloat16, jnp.float32
NT = (((1,), (1,)), ((), ()))
TN = (((0,), (0,)), ((), ()))


def act(gate, up):
    return jax.nn.gelu(gate) * up


def kernel(
    n, x_ref, dy_ref, gate_ref, up_ref, wg_ref, wu_ref, wd_ref,
    dx_ref, dwg_ref, dwu_ref, dwd_ref, dyg, xg, pbuf,
    wd_v, wgu_v, dgu_v, hid_v, tile_v, gu_v, dh_v, psend, rsend, rrecv, acc_v, strip_v, so_v, sd_v,
    ag_s, ag_r, p_s, p_r, q_s, q_r, w_sem, g_sem, t_sem, own_sem, st_sem, so_sem, sd_sem, dx_sem,
):
    me = lax.axis_index("tp")
    core = lax.rem(me, 2)
    other = 1 - 2 * core
    right, left, far = lax.rem(me + 2, n), lax.rem(me + n - 2, n), lax.rem(me + 4, n)
    partner = me + other
    R, D = dy_ref.shape
    H = R // 2
    F = gate_ref.shape[1]
    T = n * R

    def rows(block, half=None):
        if half is None:
            return pl.ds(pl.multiple_of(block * R, R), R)
        return pl.ds(pl.multiple_of(block * R + half * H, H), H)

    def local(src, dst, sem):
        return pltpu.make_async_copy(src, dst, sem)

    def remote(src, dst, s, r, to):
        return pltpu.make_async_remote_copy(src_ref=src, dst_ref=dst, send_sem=s, recv_sem=r, device_id={"tp": to}, device_id_type=MESH)

    pieces = ((left, 0), (left, 1), (right, 1), (right, 0), (far, 0), (far, 1))
    own_sends = ((right, 0), (right, 1), (left, 1), (left, 0))
    own = (dy_ref, x_ref)
    full = (dyg, xg)

    def ring_own(a, k):
        to, half = own_sends[k]
        return remote(own[a].at[pl.ds(half * H, H)], full[a].at[rows(me, half)], ag_s.at[a, k], ag_r.at[a, k], to)

    def ring_fwd(a, k):
        block, half, to = ((left, 0, right), (right, 1, left))[k - 4]
        ref = full[a].at[rows(block, half)]
        return remote(ref, ref, ag_s.at[a, k], ag_r.at[a, k], to)

    def ring_arrived(a, k):
        block, half = pieces[k]
        ref = full[a].at[rows(block, half)]
        remote(ref, ref, ag_s.at[a, k], ag_r.at[a, k], partner).wait_recv()

    def pair_own(a):
        return remote(own[a], full[a].at[rows(me)], ag_s.at[a, 6], ag_r.at[a, 6], partner)

    def pair_fwd(a, k):
        block, half = pieces[k]
        ref = full[a].at[rows(block, half)]
        return remote(ref, ref, ag_s.at[a, 7 + k], ag_r.at[a, 7 + k], partner)

    def pair_arrived(a, k):
        if k < 0:
            ref = full[a].at[rows(partner)]
            remote(ref, ref, ag_s.at[a, 6], ag_r.at[a, 6], partner).wait_recv()
        else:
            block, half = pieces[k]
            ref = full[a].at[rows(block + other, half)]
            remote(ref, ref, ag_s.at[a, 7 + k], ag_r.at[a, 7 + k], partner).wait_recv()

    w_copies = (
        local(wd_ref, wd_v, w_sem.at[0]),
        local(wg_ref, wgu_v.at[:, pl.ds(0, F)], w_sem.at[1]),
        local(wu_ref, wgu_v.at[:, pl.ds(F, F)], w_sem.at[2]),
    )

    barrier = pltpu.get_barrier_semaphore()
    for to in (left, right, partner):
        pl.semaphore_signal(barrier, inc=1, device_id={"tp": to}, device_id_type=MESH)
    pl.semaphore_wait(barrier, 3)

    for k in (0, 2, 1, 3):
        ring_own(0, k).start()
    pair_own(0).start()
    pair_own(1).start()

    def block_of(s):
        j = s // 2
        hop = j + j // 2 - 2 * (j // 3)
        return lax.rem(me + 2 * hop, n) + lax.rem(s, 2) * other

    def gate_load(s, slot):
        r = rows(block_of(s))
        return (
            local(gate_ref.at[r], gu_v.at[slot, 0], g_sem.at[slot, 0]),
            local(up_ref.at[r], gu_v.at[slot, 1], g_sem.at[slot, 1]),
        )

    def tile_load(s, slot):
        return local(dyg.at[rows(block_of(s))], tile_v.at[slot], t_sem.at[slot])

    w_copies[0].start()
    local(dy_ref, tile_v.at[0], t_sem.at[0]).start()
    for c in gate_load(0, 0):
        c.start()
    stage = [local(dy_ref, psend.at[0], own_sem.at[0]), local(x_ref, psend.at[1], own_sem.at[1])]
    for c in stage:
        c.start()
    w_copies[1].start()
    w_copies[2].start()
    for c in stage:
        c.wait()
    stage = [local(psend.at[0], dyg.at[rows(me)], own_sem.at[0]), local(psend.at[1], xg.at[rows(me)], own_sem.at[1])]
    for c in stage:
        c.start()
    w_copies[0].wait()

    def step(s, _):
        slot, nxt = lax.rem(s, 2), lax.rem(s + 1, 2)
        r = rows(block_of(s))
        tile_load(s, slot).wait()
        for c in gate_load(s, slot):
            c.wait()
        dh_v[...] = lax.dot_general(tile_v[slot], wd_v[...], NT, preferred_element_type=F32)

        @pl.when(s == 0)
        def _():
            pair_arrived(0, -1)

        @pl.when(s == 1)
        def _():
            for k in (0, 2):
                ring_arrived(0, k)
            for k in (4, 5):
                ring_fwd(0, k).start()
            for k in (0, 2, 1, 3):
                ring_own(1, k).start()
            for k in (0, 2):
                pair_fwd(0, k).start()
            for k in (1, 3):
                ring_arrived(0, k)
                pair_fwd(0, k).start()

        @pl.when(s == 2)
        def _():
            for k in (2, 3):
                pair_arrived(0, k)

        @pl.when(s == 4)
        def _():
            for k in (0, 1):
                pair_arrived(0, k)

        @pl.when(s == 5)
        def _():
            for k in (4, 5):
                ring_arrived(0, k)
                pair_fwd(0, k).start()

        @pl.when(s == 6)
        def _():
            for k in (4, 5):
                pair_arrived(0, k)

        @pl.when(s < n - 1)
        def _():
            tile_load(s + 1, nxt).start()
            for c in gate_load(s + 1, nxt):
                c.start()

        def chunk(i, _):
            m = 16
            q = pl.ds(pl.multiple_of(i * m, m), m)
            o = pl.ds(pl.multiple_of(block_of(s) * R + i * m, m), m)
            hidden, back = jax.vjp(act, gu_v[slot, 0, q].astype(F32), gu_v[slot, 1, q].astype(F32))
            dg, du = back(dh_v[q])
            dgu_v[o, pl.ds(0, F)] = dg.astype(BF16)
            dgu_v[o, pl.ds(F, F)] = du.astype(BF16)
            hid_v[o] = hidden.astype(BF16)
            return 0

        lax.fori_loop(0, R // 16, chunk, 0)
        return 0

    lax.fori_loop(0, n, step, 0)
    for c in stage:
        c.wait()
    for c in w_copies[1:]:
        c.wait()

    NB = 512

    def dx_terms(row0, m, emit):
        def ntile(t, _):
            cols = pl.ds(pl.multiple_of(t * NB, NB), NB)
            emit(cols, lax.dot_general(dgu_v[pl.ds(row0, m)], wgu_v[cols], NT, preferred_element_type=F32))
            return 0

        lax.fori_loop(0, D // NB, ntile, 0)

    targets = (far, right, left, me)

    def p_copy(i):
        return remote(psend.at[i % 2], pbuf.at[i], p_s.at[i], p_r.at[i], partner)

    for i, block in enumerate(targets):
        if i >= 2:
            p_copy(i - 2).wait_send()

        def emit(cols, v, i=i):
            psend[i % 2, :, cols] = v.astype(BF16)

        dx_terms(pl.multiple_of((block + other) * R, R), R, emit)
        p_copy(i).start()

    for k in (0, 2):
        ring_arrived(1, k)
    for k in (4, 5):
        ring_fwd(1, k).start()
    for k in (0, 2):
        pair_fwd(1, k).start()

    def p_load(i, half=None):
        if half is None:
            return local(pbuf.at[i], tile_v.at[i % 2], t_sem.at[i % 2])
        h = pl.ds(half * H, H)
        return local(pbuf.at[i, h], tile_v.at[i % 2, h], t_sem.at[i % 2])

    def p_fetch(i):
        p_copy(i).wait_recv()
        p_load(i).start()

    def q_sub(q, sub, subs):
        to = (right, left)[q % 2]
        h = pl.ds(sub * (H // subs), H // subs)
        k = q + 2 * sub
        return remote(rsend.at[q, h], rrecv.at[q, h], q_s.at[k], q_r.at[k], to)

    def q_parts(q):
        return [q_sub(q, sub, 2 if q >= 4 else 1) for sub in range(2 if q >= 4 else 1)]

    def ring_sum(q, i, half, add=None):
        h = pl.ds(half * H, H)

        def emit(cols, v):
            v = v + tile_v[i % 2, h, cols].astype(F32)
            if add is not None:
                v = v + rrecv[add, :, cols].astype(F32)
            rsend[q, :, cols] = v.astype(BF16)

        dx_terms(pl.multiple_of(targets[i] * R + half * H, H), H, emit)
        for c in q_parts(q):
            c.start()

    p_fetch(0)
    p_fetch(1)
    p_load(0).wait()
    ring_sum(0, 0, 0)
    ring_sum(1, 0, 1)
    p_fetch(2)
    p_load(1).wait()
    ring_sum(2, 1, 1)
    p_fetch(3)
    p_load(2).wait()
    ring_sum(3, 2, 0)
    p_load(3).wait()

    def emit_own(cols, v):
        acc_v[:, cols] = v + tile_v[1, :, cols].astype(F32)

    dx_terms(pl.multiple_of(me * R, R), R, emit_own)

    for k in (1, 3):
        ring_arrived(1, k)
        pair_fwd(1, k).start()

    W = strip_v.shape[2]

    def strip_load(a, t, slot):
        return local(full[a].at[:, pl.ds(pl.multiple_of(t * W, W), W)], strip_v.at[slot], st_sem.at[slot])

    def strips(a, lo, hi, out, work):
        strip_load(a, lo, lo % 2).start()

        def one(t, _):
            slot = lax.rem(t, 2)
            strip_load(a, t, slot).wait()

            @pl.when(t + 1 < hi)
            def _():
                strip_load(a, t + 1, 1 - slot).start()

            @pl.when(t >= lo + 2)
            def _():
                for c in out(t - 2, slot):
                    c.wait()

            work(slot)
            for c in out(t, slot):
                c.start()
            return 0

        lax.fori_loop(lo, hi, one, 0)
        for t in (hi - 2, hi - 1):
            for c in out(t, t % 2):
                c.wait()

    def down_out(t, slot):
        return (local(sd_v.at[slot], dwd_ref.at[:, pl.ds(pl.multiple_of(t * W, W), W)], sd_sem.at[slot]),)

    def down_work(slot):
        v = lax.dot_general(strip_v[slot], hid_v[...], TN, preferred_element_type=F32)
        sd_v[slot] = v.T.astype(BF16)

    def in_out(t, slot):
        r = pl.ds(pl.multiple_of(t * W, W), W)
        return (
            local(so_v.at[slot, :, pl.ds(0, F)], dwg_ref.at[r], so_sem.at[slot, 0]),
            local(so_v.at[slot, :, pl.ds(F, F)], dwu_ref.at[r], so_sem.at[slot, 1]),
        )

    def in_work(slot):
        v = lax.dot_general(strip_v[slot], dgu_v[...], TN, preferred_element_type=F32)
        so_v[slot] = v.astype(BF16)

    S = D // W
    strips(0, 0, S, down_out, down_work)

    for k in (4, 5):
        ring_arrived(1, k)
        pair_fwd(1, k).start()
    for k in (-1, 0, 1, 2, 3, 4, 5):
        pair_arrived(1, k)

    strips(1, 0, S // 2, in_out, in_work)

    for i, half in ((1, 0), (2, 1)):
        p_load(i, half).start()
    for c in q_parts(0) + q_parts(1):
        c.wait_recv()
    for i, half in ((1, 0), (2, 1)):
        p_load(i, half).wait()
    ring_sum(4, 1, 0, add=0)
    ring_sum(5, 2, 1, add=1)

    strips(1, S // 2, S, in_out, in_work)

    def add_rows(lo, m, srcs):
        def chunk(i, _):
            r = pl.ds(pl.multiple_of(lo + i * 16, 16), 16)
            v = acc_v[r]
            for q in srcs:
                v = v + rrecv[q, pl.ds(pl.multiple_of(lo % H + i * 16, 16), 16)].astype(F32)
            return r, v

        return chunk

    for c in q_parts(2) + q_parts(3):
        c.wait_recv()

    outs = []
    for sub in range(2):
        for q, first, base in ((4, 3, 0), (5, 2, H)):
            q_parts(q)[sub].wait_recv()
            lo = base + sub * (H // 2)
            chunk = add_rows(lo, H // 2, (first, q))

            def put(i, _, chunk=chunk):
                r, v = chunk(i, _)
                tile_v[0, r] = v.astype(BF16)
                return 0

            lax.fori_loop(0, H // 2 // 16, put, 0)
            r = pl.ds(lo, H // 2)
            out = local(tile_v.at[0, r], dx_ref.at[r], dx_sem.at[len(outs)])
            out.start()
            outs.append(out)

    for a in range(2):
        for k in range(4):
            ring_own(a, k).wait_send()
        for k in (4, 5):
            ring_fwd(a, k).wait_send()
        pair_own(a).wait_send()
        for k in range(6):
            pair_fwd(a, k).wait_send()
    for i in (2, 3):
        p_copy(i).wait_send()
    for q in range(6):
        for c in q_parts(q):
            c.wait_send()
    for c in outs:
        c.wait()


def solution(mesh):
    n = mesh.shape["tp"]

    def body(x, dy, gate, up, w_gate, w_up, w_down):
        R, D = x.shape
        T, F = gate.shape
        H = R // 2
        W = 256
        out = lambda *s: jax.ShapeDtypeStruct(s, BF16)
        any_spec = pl.BlockSpec(memory_space=pl.ANY)
        dma = pltpu.SemaphoreType.DMA
        res = pl.pallas_call(
            functools.partial(kernel, n),
            out_shape=[out(R, D), out(D, F), out(D, F), out(F, D), out(T, D), out(T, D), out(4, R, D)],
            in_specs=[any_spec] * 7,
            out_specs=[any_spec] * 7,
            scratch_shapes=[
                pltpu.VMEM((F, D), BF16),
                pltpu.VMEM((D, 2 * F), BF16),
                pltpu.VMEM((T, 2 * F), BF16),
                pltpu.VMEM((T, F), BF16),
                pltpu.VMEM((2, R, D), BF16),
                pltpu.VMEM((2, 2, R, F), BF16),
                pltpu.VMEM((R, F), F32),
                pltpu.VMEM((2, R, D), BF16),
                pltpu.VMEM((6, H, D), BF16),
                pltpu.VMEM((6, H, D), BF16),
                pltpu.VMEM((R, D), F32),
                pltpu.VMEM((2, T, W), BF16),
                pltpu.VMEM((2, W, 2 * F), BF16),
                pltpu.VMEM((2, F, W), BF16),
                dma((2, 13)), dma((2, 13)),
                dma((4,)), dma((4,)),
                dma((8,)), dma((8,)),
                dma((3,)), dma((2, 2)), dma((2,)), dma((2,)),
                dma((2,)), dma((2, 2)), dma((2,)), dma((4,)),
            ],
            compiler_params=pltpu.CompilerParams(collective_id=0, has_side_effects=True, vmem_limit_bytes=67043328),
            name="mlp_backward",
        )(x, dy, gate, up, w_gate, w_up, w_down)
        return tuple(res[:4])

    tok, col, row = P(("dp", "tp"), None), P("dp", "tp"), P("tp", None)
    wcol = P(None, "tp")
    return jax.shard_map(
        body, mesh=mesh, in_specs=(tok, tok, col, col, wcol, wcol, row), out_specs=(tok, col, col, tok), check_vma=False
    )
```

time: 275 us -> 221 us (0.80)
  Pallas kernels: 0 us -> 210 us
  matrix products: 132 us -> 0 us
  waiting for transfers between devices: 124 us -> 0 us
  between operations: 13.8 us -> 0.65 us
  local copies, waits for them, and re-layouts: 5.16 us -> 10.2 us
    pallas_call x0 -> x1, Pallas kernels: none -> 210 us  [body(): pl.pallas_call(functools.partial(kernel, n), out_shape=[out(R, D), out(D,...]
    dot_general x6 -> x0, matrix products: 132 us -> none  [the longest x3 59.8 us: by_group(): jnp.einsum('gta,gtb->gab', a, b, preferred_element_type=jnp.float32)]
    unnamed x5 -> x0, waiting for transfers between devices: 113 us -> none
    reshape x1 -> x0, waiting for transfers between devices: 11.4 us -> none  [by_group(): a, b = (t.reshape(groups, -1, t.shape[-1]) for t in (a, b))]
    unnamed x6 -> x10, local copies, waits for them, and re-layouts: 5.16 us -> 10.2 us
  transfers between devices with their start and end apart: 3 -> 0, of which waited for: 3 -> 0; matrix products, arithmetic and copies ran while one was open for 50% -> 0% of each run, Pallas kernels for 0% -> 0%
where the time goes in v1:
time: 221 us; the launch traced here: 220 us
  Pallas kernels  210 us (95%)
  local copies, waits for them, and re-layouts  10.2 us (5%)
    pallas_call x1, Pallas kernels, body(): pl.pallas_call(functools.partial(kernel, n), out_shape=[out(R, D), out(D,...  210 us
    unnamed x10, local copies, waits for them, and re-layouts  10.2 us

profile of v1, /device:TPU:112, one launch (start us, length us, event | category | flops | bytes accessed | tf_op | source)
XLA Modules:
  0.0 220.5 jit_solution(5068017335988126364)
XLA Ops:
  0.6 209.6 %mlp_backward.1 = (bf16[512,2048]{1,0:T(8,128)(2,1)}, bf16[2048,640]{1,0:T(8,128)(2,1)}, bf16[2048,640]{1,0:T(8,128)(2,1)}, bf16[640,2048]{1,0:T(8,128)(2,1)}, b...) custom-call(bf16[512,2048]{1,0:T(8,128)(2,1)} %x_ref.1, ...), custom_call_target="tpu_custom_call" | custom-call | tf_op jit(solution)/shard_map/mlp_backward/pallas_call | solution.py:419
  210.3 0.0 copy-start.2
  210.3 3.3 %copy.15 = bf16[512,2048]{1,0:T(8,128)(2,1)} copy(bf16[512,2048]{1,0:T(8,128)(2,1)} %get-tuple-element.16) | data formatting | bytes 4194304
  213.6 0.0 copy-done.2
  213.6 0.0 copy-start.1
  213.6 1.5 copy.16
  215.1 1.2 copy-done.1
  216.3 0.0 copy-start
  216.3 1.5 copy.17
  217.8 1.2 copy-done
  219.0 1.5 copy.18
Async XLA Ops:
  210.3 3.3 %copy-start.2 = (bf16[2048,640]{1,0:T(8,128)(2,1)S(1)}, bf16[2048,640]{1,0:T(8,128)(2,1)}, u32[]{:S(2)}) copy-start(bf16[2048,640]{1,0:T(8,128)(2,1)} %get-tuple-element.17) | copy-start | bytes 7864324
  213.6 2.7 %copy-start.1 = (bf16[2048,640]{1,0:T(8,128)(2,1)S(1)}, bf16[2048,640]{1,0:T(8,128)(2,1)}, u32[]{:S(2)}) copy-start(bf16[2048,640]{1,0:T(8,128)(2,1)} %get-tuple-element.18) | copy-start | bytes 7864324
  216.3 2.7 %copy-start = (bf16[640,2048]{1,0:T(8,128)(2,1)S(1)}, bf16[640,2048]{1,0:T(8,128)(2,1)}, u32[]{:S(2)}) copy-start(bf16[640,2048]{1,0:T(8,128)(2,1)} %get-tuple-element.19) | copy-start | bytes 7864324

commit v2 on v1

--- a/solution.py
+++ b/solution.py
@@ -20,8 +20,8 @@
 def kernel(
     n, x_ref, dy_ref, gate_ref, up_ref, wg_ref, wu_ref, wd_ref,
     dx_ref, dwg_ref, dwu_ref, dwd_ref, dyg, xg, pbuf,
-    wd_v, wgu_v, dgu_v, hid_v, tile_v, gu_v, dh_v, psend, rsend, rrecv, acc_v, strip_v, so_v, sd_v,
-    ag_s, ag_r, p_s, p_r, q_s, q_r, w_sem, g_sem, t_sem, own_sem, st_sem, so_sem, sd_sem, dx_sem,
+    wgu_v, dgu_v, hid_v, tile_v, gu_v, dh_v, psend, rsend, rrecv, acc_v, strip_v,
+    ag_s, ag_r, p_s, p_r, q_s, q_r, w_sem, g_sem, t_sem, own_sem, st_sem, dx_sem,
 ):
     me = lax.axis_index("tp")
     core = lax.rem(me, 2)
@@ -46,7 +46,7 @@
 
     pieces = ((left, 0), (left, 1), (right, 1), (right, 0), (far, 0), (far, 1))
     own_sends = ((right, 0), (right, 1), (left, 1), (left, 0))
-    own = (dy_ref, x_ref)
+    own = (psend.at[0], x_ref)
     full = (dyg, xg)
 
     def ring_own(a, k):
@@ -80,17 +80,24 @@
             ref = full[a].at[rows(block + other, half)]
             remote(ref, ref, ag_s.at[a, 7 + k], ag_r.at[a, 7 + k], partner).wait_recv()
 
+    wd_v = dwd_ref
     w_copies = (
         local(wd_ref, wd_v, w_sem.at[0]),
         local(wg_ref, wgu_v.at[:, pl.ds(0, F)], w_sem.at[1]),
         local(wu_ref, wgu_v.at[:, pl.ds(F, F)], w_sem.at[2]),
     )
 
+    stage = [local(dy_ref.at[pl.ds(h * H, H)], psend.at[0, pl.ds(h * H, H)], dx_sem.at[h]) for h in range(2)]
+    for c in stage:
+        c.start()
+
     barrier = pltpu.get_barrier_semaphore()
     for to in (left, right, partner):
         pl.semaphore_signal(barrier, inc=1, device_id={"tp": to}, device_id_type=MESH)
     pl.semaphore_wait(barrier, 3)
 
+    for c in stage:
+        c.wait()
     for k in (0, 2, 1, 3):
         ring_own(0, k).start()
     pair_own(0).start()
@@ -115,13 +122,11 @@
     local(dy_ref, tile_v.at[0], t_sem.at[0]).start()
     for c in gate_load(0, 0):
         c.start()
-    stage = [local(dy_ref, psend.at[0], own_sem.at[0]), local(x_ref, psend.at[1], own_sem.at[1])]
-    for c in stage:
-        c.start()
+    x_stage = local(x_ref, psend.at[1], own_sem.at[1])
+    x_stage.start()
     w_copies[1].start()
     w_copies[2].start()
-    for c in stage:
-        c.wait()
+    x_stage.wait()
     stage = [local(psend.at[0], dyg.at[rows(me)], own_sem.at[0]), local(psend.at[1], xg.at[rows(me)], own_sem.at[1])]
     for c in stage:
         c.start()
@@ -215,6 +220,9 @@
     def p_copy(i):
         return remote(psend.at[i % 2], pbuf.at[i], p_s.at[i], p_r.at[i], partner)
 
+    for k in range(4):
+        ring_own(0, k).wait_send()
+    pair_own(0).wait_send()
     for i, block in enumerate(targets):
         if i >= 2:
             p_copy(i - 2).wait_send()
@@ -242,27 +250,32 @@
         p_copy(i).wait_recv()
         p_load(i).start()
 
-    def q_sub(q, sub, subs):
-        to = (right, left)[q % 2]
-        h = pl.ds(sub * (H // subs), H // subs)
-        k = q + 2 * sub
-        return remote(rsend.at[q, h], rrecv.at[q, h], q_s.at[k], q_r.at[k], to)
+    cuts = (0, H // 2, 3 * H // 4, 7 * H // 8, H)
+
+    def q_src(q):
+        return rsend.at[q] if q < 4 else psend.at[0, pl.ds((q - 4) * H, H)]
+
+    def q_part(q, sub=None):
+        lo, hi, k = (0, H, q) if sub is None else (cuts[sub], cuts[sub + 1], q + 2 * sub)
+        h = pl.ds(lo, hi - lo)
+        return remote(q_src(q).at[h], rrecv.at[q, h], q_s.at[k], q_r.at[k], (right, left)[q % 2])
 
     def q_parts(q):
-        return [q_sub(q, sub, 2 if q >= 4 else 1) for sub in range(2 if q >= 4 else 1)]
+        return [q_part(q)] if q < 4 else [q_part(q, sub) for sub in range(4)]
 
     def ring_sum(q, i, half, add=None):
         h = pl.ds(half * H, H)
+        dst = q_src(q)
 
         def emit(cols, v):
             v = v + tile_v[i % 2, h, cols].astype(F32)
             if add is not None:
                 v = v + rrecv[add, :, cols].astype(F32)
-            rsend[q, :, cols] = v.astype(BF16)
+            dst[:, cols] = v.astype(BF16)
 
         dx_terms(pl.multiple_of(targets[i] * R + half * H, H), H, emit)
-        for c in q_parts(q):
-            c.start()
+        if q < 4:
+            q_part(q).start()
 
     p_fetch(0)
     p_fetch(1)
@@ -291,7 +304,7 @@
     def strip_load(a, t, slot):
         return local(full[a].at[:, pl.ds(pl.multiple_of(t * W, W), W)], strip_v.at[slot], st_sem.at[slot])
 
-    def strips(a, lo, hi, out, work):
+    def strips(a, lo, hi, work):
         strip_load(a, lo, lo % 2).start()
 
         def one(t, _):
@@ -302,41 +315,22 @@
             def _():
                 strip_load(a, t + 1, 1 - slot).start()
 
-            @pl.when(t >= lo + 2)
-            def _():
-                for c in out(t - 2, slot):
-                    c.wait()
-
-            work(slot)
-            for c in out(t, slot):
-                c.start()
+            work(slot, pl.ds(pl.multiple_of(t * W, W), W))
             return 0
 
         lax.fori_loop(lo, hi, one, 0)
-        for t in (hi - 2, hi - 1):
-            for c in out(t, t % 2):
-                c.wait()
-
-    def down_out(t, slot):
-        return (local(sd_v.at[slot], dwd_ref.at[:, pl.ds(pl.multiple_of(t * W, W), W)], sd_sem.at[slot]),)
-
-    def down_work(slot):
+
+    def down_work(slot, part):
         v = lax.dot_general(strip_v[slot], hid_v[...], TN, preferred_element_type=F32)
-        sd_v[slot] = v.T.astype(BF16)
-
-    def in_out(t, slot):
-        r = pl.ds(pl.multiple_of(t * W, W), W)
-        return (
-            local(so_v.at[slot, :, pl.ds(0, F)], dwg_ref.at[r], so_sem.at[slot, 0]),
-            local(so_v.at[slot, :, pl.ds(F, F)], dwu_ref.at[r], so_sem.at[slot, 1]),
-        )
-
-    def in_work(slot):
+        dwd_ref[:, part] = v.T.astype(BF16)
+
+    def in_work(slot, part):
         v = lax.dot_general(strip_v[slot], dgu_v[...], TN, preferred_element_type=F32)
-        so_v[slot] = v.astype(BF16)
+        dwg_ref[part] = v[:, :F].astype(BF16)
+        dwu_ref[part] = v[:, F:].astype(BF16)
 
     S = D // W
-    strips(0, 0, S, down_out, down_work)
+    strips(0, 0, S, down_work)
 
     for k in (4, 5):
         ring_arrived(1, k)
@@ -344,7 +338,7 @@
     for k in (-1, 0, 1, 2, 3, 4, 5):
         pair_arrived(1, k)
 
-    strips(1, 0, S // 2, in_out, in_work)
+    strips(1, 0, S // 2, in_work)
 
     for i, half in ((1, 0), (2, 1)):
         p_load(i, half).start()
@@ -352,56 +346,50 @@
         c.wait_recv()
     for i, half in ((1, 0), (2, 1)):
         p_load(i, half).wait()
+    for i in (2, 3):
+        p_copy(i).wait_send()
     ring_sum(4, 1, 0, add=0)
     ring_sum(5, 2, 1, add=1)
-
-    strips(1, S // 2, S, in_out, in_work)
-
-    def add_rows(lo, m, srcs):
-        def chunk(i, _):
-            r = pl.ds(pl.multiple_of(lo + i * 16, 16), 16)
-            v = acc_v[r]
-            for q in srcs:
-                v = v + rrecv[q, pl.ds(pl.multiple_of(lo % H + i * 16, 16), 16)].astype(F32)
-            return r, v
-
-        return chunk
-
-    for c in q_parts(2) + q_parts(3):
-        c.wait_recv()
-
-    outs = []
-    for sub in range(2):
+    for sub in range(4):
+        for q in (4, 5):
+            q_part(q, sub).start()
+
+    strips(1, S // 2, S, in_work)
+
+    for q in (2, 3):
+        q_part(q).wait_recv()
+    for sub in range(4):
         for q, first, base in ((4, 3, 0), (5, 2, H)):
-            q_parts(q)[sub].wait_recv()
-            lo = base + sub * (H // 2)
-            chunk = add_rows(lo, H // 2, (first, q))
-
-            def put(i, _, chunk=chunk):
-                r, v = chunk(i, _)
-                tile_v[0, r] = v.astype(BF16)
+            q_part(q, sub).wait_recv()
+
+            def put(i, _, q=q, first=first, base=base, lo=cuts[sub]):
+                h = pl.ds(pl.multiple_of(lo + i * 16, 16), 16)
+                r = pl.ds(pl.multiple_of(base + lo + i * 16, 16), 16)
+                v = acc_v[r] + rrecv[first, h].astype(F32) + rrecv[q, h].astype(F32)
+                dx_ref[r] = v.astype(BF16)
                 return 0
 
-            lax.fori_loop(0, H // 2 // 16, put, 0)
-            r = pl.ds(lo, H // 2)
-            out = local(tile_v.at[0, r], dx_ref.at[r], dx_sem.at[len(outs)])
-            out.start()
-            outs.append(out)
-
+            lax.fori_loop(0, (cuts[sub + 1] - cuts[sub]) // 16, put, 0)
+
+    for k in range(4):
+        ring_own(1, k).wait_send()
+    pair_own(1).wait_send()
     for a in range(2):
-        for k in range(4):
-            ring_own(a, k).wait_send()
         for k in (4, 5):
             ring_fwd(a, k).wait_send()
-        pair_own(a).wait_send()
         for k in range(6):
             pair_fwd(a, k).wait_send()
-    for i in (2, 3):
-        p_copy(i).wait_send()
     for q in range(6):
         for c in q_parts(q):
             c.wait_send()
-    for c in outs:
+
+
+def write_out(*refs):
+    k = len(refs) // 2
+    copies = [pltpu.make_async_copy(refs[i], refs[k + i], refs[-1].at[i]) for i in range(k)]
+    for c in copies:
+        c.start()
+    for c in copies:
         c.wait()
 
 
@@ -414,15 +402,16 @@
         H = R // 2
         W = 256
         out = lambda *s: jax.ShapeDtypeStruct(s, BF16)
+        results = ((R, D), (D, F), (D, F), (F, D))
+        vmem_spec = pl.BlockSpec(memory_space=pltpu.VMEM)
         any_spec = pl.BlockSpec(memory_space=pl.ANY)
         dma = pltpu.SemaphoreType.DMA
         res = pl.pallas_call(
             functools.partial(kernel, n),
-            out_shape=[out(R, D), out(D, F), out(D, F), out(F, D), out(T, D), out(T, D), out(4, R, D)],
+            out_shape=[pltpu.VMEM(s, BF16) for s in results] + [out(T, D), out(T, D), out(4, R, D)],
             in_specs=[any_spec] * 7,
-            out_specs=[any_spec] * 7,
+            out_specs=[vmem_spec] * 4 + [any_spec] * 3,
             scratch_shapes=[
-                pltpu.VMEM((F, D), BF16),
                 pltpu.VMEM((D, 2 * F), BF16),
                 pltpu.VMEM((T, 2 * F), BF16),
                 pltpu.VMEM((T, F), BF16),
@@ -430,22 +419,30 @@
                 pltpu.VMEM((2, 2, R, F), BF16),
                 pltpu.VMEM((R, F), F32),
                 pltpu.VMEM((2, R, D), BF16),
-                pltpu.VMEM((6, H, D), BF16),
+                pltpu.VMEM((4, H, D), BF16),
                 pltpu.VMEM((6, H, D), BF16),
                 pltpu.VMEM((R, D), F32),
                 pltpu.VMEM((2, T, W), BF16),
-                pltpu.VMEM((2, W, 2 * F), BF16),
-                pltpu.VMEM((2, F, W), BF16),
                 dma((2, 13)), dma((2, 13)),
                 dma((4,)), dma((4,)),
-                dma((8,)), dma((8,)),
+                dma((12,)), dma((12,)),
                 dma((3,)), dma((2, 2)), dma((2,)), dma((2,)),
-                dma((2,)), dma((2, 2)), dma((2,)), dma((4,)),
+                dma((2,)), dma((2,)),
             ],
-            compiler_params=pltpu.CompilerParams(collective_id=0, has_side_effects=True, vmem_limit_bytes=67043328),
+            compiler_params=pltpu.CompilerParams(collective_id=0, has_side_effects=True, vmem_limit_bytes=217 * 2**18),
             name="mlp_backward",
         )(x, dy, gate, up, w_gate, w_up, w_down)
-        return tuple(res[:4])
+        return tuple(
+            pl.pallas_call(
+                write_out,
+                out_shape=[out(*s) for s in results],
+                in_specs=[vmem_spec] * 4,
+                out_specs=[any_spec] * 4,
+                scratch_shapes=[dma((4,))],
+                compiler_params=pltpu.CompilerParams(vmem_limit_bytes=2**18),
+                name="write_results",
+            )(*(pltpu.with_memory_space_constraint(r, pltpu.VMEM) for r in res[:4]))
+        )
 
     tok, col, row = P(("dp", "tp"), None), P("dp", "tp"), P("tp", None)
     wcol = P(None, "tp")

time: 221 us -> 214 us (0.968)
  local copies, waits for them, and re-layouts: 10.2 us -> 0 us
  Pallas kernels: 210 us -> 213 us
    unnamed x10 -> x0, local copies, waits for them, and re-layouts: 10.2 us -> none
    pallas_call x1 -> x2, Pallas kernels: 210 us -> 213 us  [the longest x1 209 us: body(): pl.pallas_call(functools.partial(kernel, n), out_shape=[pltpu.VMEM(s, BF1...]
where the time goes in v2:
time: 214 us
  Pallas kernels  213 us (100%)
    pallas_call x1, Pallas kernels, body(): pl.pallas_call(functools.partial(kernel, n), out_shape=[pltpu.VMEM(s, BF1...  209 us

profile of v2, /device:TPU:112, one launch (start us, length us, event | category | flops | bytes accessed | tf_op | source)
XLA Modules:
  0.0 214.1 jit_solution(15749824043091848221)
XLA Ops:
  0.6 209.5 %mlp_backward.1 = (bf16[512,2048]{1,0:T(8,128)(2,1)S(1)}, bf16[2048,640]{1,0:T(8,128)(2,1)S(1)}, bf16[2048,640]{1,0:T(8,128)(2,1)S(1)}, bf16[640,2048]{1,0:T(8,1...) custom-call(bf16[512,2048]{1,0:T(8,128)(2,1)} %x_ref.1, ...), custom_call_target="tpu_custom_call" | custom-call | tf_op jit(solution)/shard_map/mlp_backward/pallas_call | solution.py:409
  210.1 3.9 %write_results.1 = (bf16[512,2048]{1,0:T(8,128)(2,1)}, bf16[2048,640]{1,0:T(8,128)(2,1)}, bf16[2048,640]{1,0:T(8,128)(2,1)}, bf16[640,2048]{1,0:T(8,128)(2,1)}) custom-call(bf16[512,2048]{1,0:T(8,128)(2,1)S(1)} %get-tuple-element.8.refs_0_, bf16[2048,640]{1,0:T(8,128)(2,1)S(1)} %get-tuple-element.9.refs_1_, bf16[2048,640]{1,0:T(8,128)(2,1)S(1)} %get-tuple-element.10.refs_2_, ...), custom_call_target="tpu_custom_call" | custom-call | tf_op jit(solution)/shard_map/write_results/pallas_call | solution.py:436

commit v3 on v2

--- a/solution.py
+++ b/solution.py
@@ -21,7 +21,7 @@
     n, x_ref, dy_ref, gate_ref, up_ref, wg_ref, wu_ref, wd_ref,
     dx_ref, dwg_ref, dwu_ref, dwd_ref, dyg, xg, pbuf,
     wgu_v, dgu_v, hid_v, tile_v, gu_v, dh_v, psend, rsend, rrecv, acc_v, strip_v,
-    ag_s, ag_r, p_s, p_r, q_s, q_r, w_sem, g_sem, t_sem, own_sem, st_sem, dx_sem,
+    ag_s, ag_r, p_s, p_r, q_s, q_r, w_sem, g_sem, t_sem, own_sem, st_sem,
 ):
     me = lax.axis_index("tp")
     core = lax.rem(me, 2)
@@ -46,7 +46,7 @@
 
     pieces = ((left, 0), (left, 1), (right, 1), (right, 0), (far, 0), (far, 1))
     own_sends = ((right, 0), (right, 1), (left, 1), (left, 0))
-    own = (psend.at[0], x_ref)
+    own = (dy_ref, x_ref)
     full = (dyg, xg)
 
     def ring_own(a, k):
@@ -87,17 +87,11 @@
         local(wu_ref, wgu_v.at[:, pl.ds(F, F)], w_sem.at[2]),
     )
 
-    stage = [local(dy_ref.at[pl.ds(h * H, H)], psend.at[0, pl.ds(h * H, H)], dx_sem.at[h]) for h in range(2)]
-    for c in stage:
-        c.start()
-
     barrier = pltpu.get_barrier_semaphore()
     for to in (left, right, partner):
         pl.semaphore_signal(barrier, inc=1, device_id={"tp": to}, device_id_type=MESH)
     pl.semaphore_wait(barrier, 3)
 
-    for c in stage:
-        c.wait()
     for k in (0, 2, 1, 3):
         ring_own(0, k).start()
     pair_own(0).start()
@@ -122,11 +116,13 @@
     local(dy_ref, tile_v.at[0], t_sem.at[0]).start()
     for c in gate_load(0, 0):
         c.start()
-    x_stage = local(x_ref, psend.at[1], own_sem.at[1])
-    x_stage.start()
+    stage = [local(dy_ref, psend.at[0], own_sem.at[0]), local(x_ref, psend.at[1], own_sem.at[1])]
+    for c in stage:
+        c.start()
     w_copies[1].start()
     w_copies[2].start()
-    x_stage.wait()
+    for c in stage:
+        c.wait()
     stage = [local(psend.at[0], dyg.at[rows(me)], own_sem.at[0]), local(psend.at[1], xg.at[rows(me)], own_sem.at[1])]
     for c in stage:
         c.start()
@@ -220,9 +216,6 @@
     def p_copy(i):
         return remote(psend.at[i % 2], pbuf.at[i], p_s.at[i], p_r.at[i], partner)
 
-    for k in range(4):
-        ring_own(0, k).wait_send()
-    pair_own(0).wait_send()
     for i, block in enumerate(targets):
         if i >= 2:
             p_copy(i - 2).wait_send()
@@ -250,18 +243,18 @@
         p_copy(i).wait_recv()
         p_load(i).start()
 
-    cuts = (0, H // 2, 3 * H // 4, 7 * H // 8, H)
+    C = 8
+    PIECE = H // C
 
     def q_src(q):
         return rsend.at[q] if q < 4 else psend.at[0, pl.ds((q - 4) * H, H)]
 
     def q_part(q, sub=None):
-        lo, hi, k = (0, H, q) if sub is None else (cuts[sub], cuts[sub + 1], q + 2 * sub)
-        h = pl.ds(lo, hi - lo)
+        h, k = (pl.ds(0, H), q) if sub is None else (pl.ds(pl.multiple_of(sub * PIECE, PIECE), PIECE), q + 2 * sub)
         return remote(q_src(q).at[h], rrecv.at[q, h], q_s.at[k], q_r.at[k], (right, left)[q % 2])
 
     def q_parts(q):
-        return [q_part(q)] if q < 4 else [q_part(q, sub) for sub in range(4)]
+        return [q_part(q)] if q < 4 else [q_part(q, sub) for sub in range(C)]
 
     def ring_sum(q, i, half, add=None):
         h = pl.ds(half * H, H)
@@ -350,38 +343,42 @@
         p_copy(i).wait_send()
     ring_sum(4, 1, 0, add=0)
     ring_sum(5, 2, 1, add=1)
-    for sub in range(4):
+    for sub in range(C):
         for q in (4, 5):
             q_part(q, sub).start()
 
     strips(1, S // 2, S, in_work)
 
-    for q in (2, 3):
-        q_part(q).wait_recv()
-    for sub in range(4):
-        for q, first, base in ((4, 3, 0), (5, 2, H)):
-            q_part(q, sub).wait_recv()
-
-            def put(i, _, q=q, first=first, base=base, lo=cuts[sub]):
-                h = pl.ds(pl.multiple_of(lo + i * 16, 16), 16)
-                r = pl.ds(pl.multiple_of(base + lo + i * 16, 16), 16)
-                v = acc_v[r] + rrecv[first, h].astype(F32) + rrecv[q, h].astype(F32)
-                dx_ref[r] = v.astype(BF16)
-                return 0
-
-            lax.fori_loop(0, (cuts[sub + 1] - cuts[sub]) // 16, put, 0)
-
-    for k in range(4):
-        ring_own(1, k).wait_send()
-    pair_own(1).wait_send()
     for a in range(2):
+        for k in range(4):
+            ring_own(a, k).wait_send()
+        pair_own(a).wait_send()
         for k in (4, 5):
             ring_fwd(a, k).wait_send()
         for k in range(6):
             pair_fwd(a, k).wait_send()
-    for q in range(6):
-        for c in q_parts(q):
-            c.wait_send()
+    for q in range(4):
+        q_part(q).wait_send()
+    for q in (2, 3):
+        q_part(q).wait_recv()
+
+    def finish(sub, _):
+        for q, first, base in ((4, 3, 0), (5, 2, H)):
+            q_part(q, sub).wait_recv()
+
+            def put(i, _):
+                h = pl.ds(pl.multiple_of(sub * PIECE + i * 16, 16), 16)
+                r = pl.ds(pl.multiple_of(base + sub * PIECE + i * 16, 16), 16)
+                v = acc_v[r] + rrecv[first, h].astype(F32) + rrecv[q, h].astype(F32)
+                dx_ref[r] = v.astype(BF16)
+                return 0
+
+            lax.fori_loop(0, PIECE // 16, put, 0)
+        for q in (4, 5):
+            q_part(q, sub).wait_send()
+        return 0
+
+    lax.fori_loop(0, C, finish, 0)
 
 
 def write_out(*refs):
@@ -425,9 +422,9 @@
                 pltpu.VMEM((2, T, W), BF16),
                 dma((2, 13)), dma((2, 13)),
                 dma((4,)), dma((4,)),
-                dma((12,)), dma((12,)),
+                dma((20,)), dma((20,)),
                 dma((3,)), dma((2, 2)), dma((2,)), dma((2,)),
-                dma((2,)), dma((2,)),
+                dma((2,)),
             ],
             compiler_params=pltpu.CompilerParams(collective_id=0, has_side_effects=True, vmem_limit_bytes=217 * 2**18),
             name="mlp_backward",

time: 214 us -> 214 us (level)
  no operation moved by 1% of the time
where the time goes in v3:
time: 214 us; the launch traced here: 213 us
  Pallas kernels  213 us (100%)
    pallas_call x1, Pallas kernels, body(): pl.pallas_call(functools.partial(kernel, n), out_shape=[pltpu.VMEM(s, BF1...  209 us

profile of v3, /device:TPU:112, one launch (start us, length us, event | category | flops | bytes accessed | tf_op | source)
XLA Modules:
  0.0 213.3 jit_solution(15748752180665788611)
XLA Ops:
  0.6 208.7 %mlp_backward.1 = (bf16[512,2048]{1,0:T(8,128)(2,1)S(1)}, bf16[2048,640]{1,0:T(8,128)(2,1)S(1)}, bf16[2048,640]{1,0:T(8,128)(2,1)S(1)}, bf16[640,2048]{1,0:T(8,1...) custom-call(bf16[512,2048]{1,0:T(8,128)(2,1)} %x_ref.1, ...), custom_call_target="tpu_custom_call" | custom-call | tf_op jit(solution)/shard_map/mlp_backward/pallas_call | solution.py:406
  209.3 3.9 %write_results.1 = (bf16[512,2048]{1,0:T(8,128)(2,1)}, bf16[2048,640]{1,0:T(8,128)(2,1)}, bf16[2048,640]{1,0:T(8,128)(2,1)}, bf16[640,2048]{1,0:T(8,128)(2,1)}) custom-call(bf16[512,2048]{1,0:T(8,128)(2,1)S(1)} %get-tuple-element.8.refs_0_, bf16[2048,640]{1,0:T(8,128)(2,1)S(1)} %get-tuple-element.9.refs_1_, bf16[2048,640]{1,0:T(8,128)(2,1)S(1)} %get-tuple-element.10.refs_2_, ...), custom_call_target="tpu_custom_call" | custom-call | tf_op jit(solution)/shard_map/write_results/pallas_call | solution.py:433

commit v4 on v3

--- a/solution.py
+++ b/solution.py
@@ -11,6 +11,7 @@
 BF16, F32 = jnp.bfloat16, jnp.float32
 NT = (((1,), (1,)), ((), ()))
 TN = (((0,), (0,)), ((), ()))
+C = 8
 
 
 def act(gate, up):
@@ -18,9 +19,9 @@
 
 
 def kernel(
-    n, x_ref, dy_ref, gate_ref, up_ref, wg_ref, wu_ref, wd_ref,
-    dx_ref, dwg_ref, dwu_ref, dwd_ref, dyg, xg, pbuf,
-    wgu_v, dgu_v, hid_v, tile_v, gu_v, dh_v, psend, rsend, rrecv, acc_v, strip_v,
+    n, early, x_ref, dy_ref, gate_ref, up_ref, wg_ref, wu_ref, wd_ref,
+    dwg_ref, dwu_ref, dwd_ref, acc_v, last_v, dyg, xg, pbuf,
+    wgu_v, dgu_v, hid_v, tile_v, gu_v, dh_v, psend, rsend, rrecv, strip_v,
     ag_s, ag_r, p_s, p_r, q_s, q_r, w_sem, g_sem, t_sem, own_sem, st_sem,
 ):
     me = lax.axis_index("tp")
@@ -243,11 +244,10 @@
         p_copy(i).wait_recv()
         p_load(i).start()
 
-    C = 8
     PIECE = H // C
 
     def q_src(q):
-        return rsend.at[q] if q < 4 else psend.at[0, pl.ds((q - 4) * H, H)]
+        return rsend.at[q] if q < 4 else last_v.at[q - 4]
 
     def q_part(q, sub=None):
         h, k = (pl.ds(0, H), q) if sub is None else (pl.ds(pl.multiple_of(sub * PIECE, PIECE), PIECE), q + 2 * sub)
@@ -343,9 +343,13 @@
         p_copy(i).wait_send()
     ring_sum(4, 1, 0, add=0)
     ring_sum(5, 2, 1, add=1)
-    for sub in range(C):
-        for q in (4, 5):
-            q_part(q, sub).start()
+
+    @pl.when(core == 1)
+    def _():
+        for sub in range(early):
+            for q in (4, 5):
+                q_part(q, sub).start()
+
 
     strips(1, S // 2, S, in_work)
 
@@ -362,27 +366,91 @@
     for q in (2, 3):
         q_part(q).wait_recv()
 
-    def finish(sub, _):
-        for q, first, base in ((4, 3, 0), (5, 2, H)):
-            q_part(q, sub).wait_recv()
-
+    def settle(i, _):
+        h = pl.ds(pl.multiple_of(i * 16, 16), 16)
+        for q, base in ((3, 0), (2, H)):
+            r = pl.ds(pl.multiple_of(base + i * 16, 16), 16)
+            acc_v[r] = acc_v[r] + rrecv[q, h].astype(F32)
+        return 0
+
+    lax.fori_loop(0, H // 16, settle, 0)
+
+    @pl.when(core == 1)
+    def _():
+        def finish(sub, _):
+            for q, base in ((4, 0), (5, H)):
+                q_part(q, sub).wait_recv()
+
+                def put(i, _):
+                    h = pl.ds(pl.multiple_of(sub * PIECE + i * 16, 16), 16)
+                    r = pl.ds(pl.multiple_of(base + sub * PIECE + i * 16, 16), 16)
+                    acc_v[r] = acc_v[r] + rrecv[q, h].astype(F32)
+                    return 0
+
+                lax.fori_loop(0, PIECE // 16, put, 0)
+            for q in (4, 5):
+                q_part(q, sub).wait_send()
+            return 0
+
+        lax.fori_loop(0, early, finish, 0)
+
+
+def last_hop(n, early, acc_v, last_v, after_ref, dx_ref, recv_v, s_sem, r_sem):
+    me = lax.axis_index("tp")
+    core = lax.rem(me, 2)
+    to = (lax.rem(me + 2, n), lax.rem(me + n - 2, n))
+    H = acc_v.shape[0] // 2
+    PIECE = H // C
+
+    barrier = pltpu.get_barrier_semaphore()
+    for t in to:
+        pl.semaphore_signal(barrier, inc=1, device_id={"tp": t}, device_id_type=MESH)
+    pl.semaphore_wait(barrier, 2)
+
+    def part(q, sub):
+        h = pl.ds(pl.multiple_of(sub * PIECE, PIECE), PIECE)
+        return pltpu.make_async_remote_copy(
+            src_ref=last_v.at[q, h], dst_ref=recv_v.at[q, h], send_sem=s_sem.at[q, sub], recv_sem=r_sem.at[q, sub],
+            device_id={"tp": to[q]}, device_id_type=MESH,
+        )
+
+    def mine(sub):
+        return sub >= core * early
+
+    for sub in range(C):
+        @pl.when(mine(sub))
+        def _():
+            for q in range(2):
+                part(q, sub).start()
+
+    def piece(sub, add):
+        for q in range(2):
             def put(i, _):
                 h = pl.ds(pl.multiple_of(sub * PIECE + i * 16, 16), 16)
-                r = pl.ds(pl.multiple_of(base + sub * PIECE + i * 16, 16), 16)
-                v = acc_v[r] + rrecv[first, h].astype(F32) + rrecv[q, h].astype(F32)
+                r = pl.ds(pl.multiple_of(q * H + sub * PIECE + i * 16, 16), 16)
+                v = acc_v[r]
+                if add:
+                    v = v + recv_v[q, h].astype(F32)
                 dx_ref[r] = v.astype(BF16)
                 return 0
 
+            if add:
+                part(q, sub).wait_recv()
             lax.fori_loop(0, PIECE // 16, put, 0)
-        for q in (4, 5):
-            q_part(q, sub).wait_send()
+            if add:
+                part(q, sub).wait_send()
+
+    def each(sub, _):
+        pl.when(mine(sub))(lambda: piece(sub, True))
+        pl.when(jnp.logical_not(mine(sub)))(lambda: piece(sub, False))
         return 0
 
-    lax.fori_loop(0, C, finish, 0)
-
-
-def write_out(*refs):
-    k = len(refs) // 2
+    lax.fori_loop(0, C, each, 0)
+
+
+def write_out(k, *refs):
+    for mark in refs[2 * k : -1]:
+        mark[...] = jnp.zeros_like(mark)
     copies = [pltpu.make_async_copy(refs[i], refs[k + i], refs[-1].at[i]) for i in range(k)]
     for c in copies:
         c.start()
@@ -398,16 +466,32 @@
         T, F = gate.shape
         H = R // 2
         W = 256
+        early = C
         out = lambda *s: jax.ShapeDtypeStruct(s, BF16)
-        results = ((R, D), (D, F), (D, F), (F, D))
         vmem_spec = pl.BlockSpec(memory_space=pltpu.VMEM)
         any_spec = pl.BlockSpec(memory_space=pl.ANY)
         dma = pltpu.SemaphoreType.DMA
-        res = pl.pallas_call(
-            functools.partial(kernel, n),
-            out_shape=[pltpu.VMEM(s, BF16) for s in results] + [out(T, D), out(T, D), out(4, R, D)],
+        vmem = lambda s, t: pltpu.VMEM(s, t)
+        keep = lambda a: pltpu.with_memory_space_constraint(a, pltpu.VMEM)
+
+        def write(arrays, marks, name):
+            k = len(arrays)
+            return pl.pallas_call(
+                functools.partial(write_out, k),
+                out_shape=[out(*a.shape) for a in arrays] + [vmem((8, 128), F32)] * marks,
+                in_specs=[vmem_spec] * k,
+                out_specs=[any_spec] * k + [vmem_spec] * marks,
+                scratch_shapes=[dma((k,))],
+                compiler_params=pltpu.CompilerParams(vmem_limit_bytes=2**18),
+                name=name,
+            )(*(keep(a) for a in arrays))
+
+        *dw, acc, last, _, _, _ = pl.pallas_call(
+            functools.partial(kernel, n, early),
+            out_shape=[vmem(s, BF16) for s in ((D, F), (D, F), (F, D))]
+            + [vmem((R, D), F32), vmem((2, H, D), BF16), out(T, D), out(T, D), out(4, R, D)],
             in_specs=[any_spec] * 7,
-            out_specs=[vmem_spec] * 4 + [any_spec] * 3,
+            out_specs=[vmem_spec] * 5 + [any_spec] * 3,
             scratch_shapes=[
                 pltpu.VMEM((D, 2 * F), BF16),
                 pltpu.VMEM((T, 2 * F), BF16),
@@ -418,28 +502,27 @@
                 pltpu.VMEM((2, R, D), BF16),
                 pltpu.VMEM((4, H, D), BF16),
                 pltpu.VMEM((6, H, D), BF16),
-                pltpu.VMEM((R, D), F32),
                 pltpu.VMEM((2, T, W), BF16),
                 dma((2, 13)), dma((2, 13)),
                 dma((4,)), dma((4,)),
-                dma((20,)), dma((20,)),
+                dma((4 + 2 * C,)), dma((4 + 2 * C,)),
                 dma((3,)), dma((2, 2)), dma((2,)), dma((2,)),
                 dma((2,)),
             ],
-            compiler_params=pltpu.CompilerParams(collective_id=0, has_side_effects=True, vmem_limit_bytes=217 * 2**18),
+            compiler_params=pltpu.CompilerParams(collective_id=0, has_side_effects=True, vmem_limit_bytes=199 * 2**18),
             name="mlp_backward",
         )(x, dy, gate, up, w_gate, w_up, w_down)
-        return tuple(
-            pl.pallas_call(
-                write_out,
-                out_shape=[out(*s) for s in results],
-                in_specs=[vmem_spec] * 4,
-                out_specs=[any_spec] * 4,
-                scratch_shapes=[dma((4,))],
-                compiler_params=pltpu.CompilerParams(vmem_limit_bytes=2**18),
-                name="write_results",
-            )(*(pltpu.with_memory_space_constraint(r, pltpu.VMEM) for r in res[:4]))
-        )
+        *dw, written = write(dw, 1, "write_weight_gradients")
+        dx = pl.pallas_call(
+            functools.partial(last_hop, n, early),
+            out_shape=vmem((R, D), BF16),
+            in_specs=[vmem_spec] * 3,
+            out_specs=vmem_spec,
+            scratch_shapes=[pltpu.VMEM((2, H, D), BF16), dma((2, C)), dma((2, C))],
+            compiler_params=pltpu.CompilerParams(collective_id=1, has_side_effects=True, vmem_limit_bytes=2**22),
+            name="last_hop",
+        )(keep(acc), keep(last), keep(written))
+        return (write([dx], 0, "write_dx")[0], *dw)
 
     tok, col, row = P(("dp", "tp"), None), P("dp", "tp"), P("tp", None)
     wcol = P(None, "tp")

time: 214 us -> 210 us (0.981)
  Pallas kernels: 213 us -> 209 us
    pallas_call x2 -> x4, Pallas kernels: 213 us -> 209 us  [the longest x1 187 us: body(): pl.pallas_call(functools.partial(kernel, n, early), out_shape=[vmem(s, BF...]
where the time goes in v4:
time: 210 us
  Pallas kernels  209 us (100%)
    pallas_call x1, Pallas kernels, body(): pl.pallas_call(functools.partial(kernel, n, early), out_shape=[vmem(s, BF...  187 us
    pallas_call x1, Pallas kernels, body(): pl.pallas_call(functools.partial(last_hop, n, early), out_shape=vmem((R,...  17.3 us
    pallas_call x2, Pallas kernels, write(): pl.pallas_call(functools.partial(write_out, k), out_shape=[out(*a.shape)...  4.58 us

profile of v4, /device:TPU:112, one launch (start us, length us, event | category | flops | bytes accessed | tf_op | source)
XLA Modules:
  0.0 210.1 jit_solution(7219952342655403445)
XLA Ops:
  0.6 187.4 %mlp_backward.1 = (bf16[2048,640]{1,0:T(8,128)(2,1)S(1)}, bf16[2048,640]{1,0:T(8,128)(2,1)S(1)}, bf16[640,2048]{1,0:T(8,128)(2,1)S(1)}, f32[512,2048]{1,0:T(8,12...) custom-call(bf16[512,2048]{1,0:T(8,128)(2,1)} %x_ref.1, ...), custom_call_target="tpu_custom_call" | custom-call | tf_op jit(solution)/shard_map/mlp_backward/pallas_call | solution.py:489
  188.0 3.2 %write_weight_gradients.1 = (bf16[2048,640]{1,0:T(8,128)(2,1)}, bf16[2048,640]{1,0:T(8,128)(2,1)}, bf16[640,2048]{1,0:T(8,128)(2,1)}, f32[8,128]{1,0:T(8,128)S(1)}) custom-call(bf16[2048,640]{1,0:T(8,128)(2,1)S(1)} %get-tuple-element.15.refs_0_, bf16[2048,640]{1,0:T(8,128)(2,1)S(1)} %get-tuple-element.16.refs_1_, bf16[640,2048]{1,0:T(8,128)(2,1)S(1)} %get-tuple-element.17.refs_2_), custom_call_target="tpu_custom_call" | custom-call | tf_op jit(solution)/shard_map/write_weight_gradients/pallas_call | solution.py:479
  191.3 17.3 %last_hop.1.refs_0_ = bf16[512,2048]{1,0:T(8,128)(2,1)S(1)} custom-call(f32[512,2048]{1,0:T(8,128)S(1)} %get-tuple-element.13.acc_v, bf16[2,256,2048]{2,1,0:T(8,128)(2,1)S(1)} %get-tuple-element.14.last_v, f32[8,128]{1,0:T(8,128)S(1)} %get-tuple-element.18.after_ref), custom_call_target="tpu_custom_call" | custom-call | tf_op jit(solution)/shard_map/last_hop/pallas_call | solution.py:516
  208.6 1.3 write_dx.1

commit v5 on v4

--- a/solution.py
+++ b/solution.py
@@ -11,7 +11,7 @@
 BF16, F32 = jnp.bfloat16, jnp.float32
 NT = (((1,), (1,)), ((), ()))
 TN = (((0,), (0,)), ((), ()))
-C = 8
+C = 4
 
 
 def act(gate, up):
@@ -19,7 +19,7 @@
 
 
 def kernel(
-    n, early, x_ref, dy_ref, gate_ref, up_ref, wg_ref, wu_ref, wd_ref,
+    n, x_ref, dy_ref, gate_ref, up_ref, wg_ref, wu_ref, wd_ref,
     dwg_ref, dwu_ref, dwd_ref, acc_v, last_v, dyg, xg, pbuf,
     wgu_v, dgu_v, hid_v, tile_v, gu_v, dh_v, psend, rsend, rrecv, strip_v,
     ag_s, ag_r, p_s, p_r, q_s, q_r, w_sem, g_sem, t_sem, own_sem, st_sem,
@@ -346,7 +346,7 @@
 
     @pl.when(core == 1)
     def _():
-        for sub in range(early):
+        for sub in range(C):
             for q in (4, 5):
                 q_part(q, sub).start()
 
@@ -392,10 +392,10 @@
                 q_part(q, sub).wait_send()
             return 0
 
-        lax.fori_loop(0, early, finish, 0)
-
-
-def last_hop(n, early, acc_v, last_v, after_ref, dx_ref, recv_v, s_sem, r_sem):
+        lax.fori_loop(0, C, finish, 0)
+
+
+def last_hop(n, acc_v, last_v, after_ref, dx_ref, recv_v, s_sem, r_sem):
     me = lax.axis_index("tp")
     core = lax.rem(me, 2)
     to = (lax.rem(me + 2, n), lax.rem(me + n - 2, n))
@@ -414,43 +414,43 @@
             device_id={"tp": to[q]}, device_id_type=MESH,
         )
 
-    def mine(sub):
-        return sub >= core * early
-
-    for sub in range(C):
-        @pl.when(mine(sub))
-        def _():
-            for q in range(2):
-                part(q, sub).start()
-
-    def piece(sub, add):
+    def finish(lo, count, add):
         for q in range(2):
             def put(i, _):
-                h = pl.ds(pl.multiple_of(sub * PIECE + i * 16, 16), 16)
-                r = pl.ds(pl.multiple_of(q * H + sub * PIECE + i * 16, 16), 16)
+                h = pl.ds(pl.multiple_of(lo + i * 16, 16), 16)
+                r = pl.ds(pl.multiple_of(q * H + lo + i * 16, 16), 16)
                 v = acc_v[r]
                 if add:
                     v = v + recv_v[q, h].astype(F32)
                 dx_ref[r] = v.astype(BF16)
                 return 0
 
-            if add:
+            lax.fori_loop(0, count // 16, put, 0)
+
+    @pl.when(core == 0)
+    def _():
+        for sub in range(C):
+            for q in range(2):
+                part(q, sub).start()
+
+        def each(sub, _):
+            for q in range(2):
                 part(q, sub).wait_recv()
-            lax.fori_loop(0, PIECE // 16, put, 0)
-            if add:
+            finish(sub * PIECE, PIECE, True)
+            for q in range(2):
                 part(q, sub).wait_send()
-
-    def each(sub, _):
-        pl.when(mine(sub))(lambda: piece(sub, True))
-        pl.when(jnp.logical_not(mine(sub)))(lambda: piece(sub, False))
-        return 0
-
-    lax.fori_loop(0, C, each, 0)
-
-
-def write_out(k, *refs):
-    for mark in refs[2 * k : -1]:
-        mark[...] = jnp.zeros_like(mark)
+            return 0
+
+        lax.fori_loop(0, C, each, 0)
+
+    @pl.when(core == 1)
+    def _():
+        finish(0, H, False)
+
+
+def write_out(*refs):
+    k = (len(refs) - 2) // 2
+    refs[-2][...] = jnp.zeros_like(refs[-2])
     copies = [pltpu.make_async_copy(refs[i], refs[k + i], refs[-1].at[i]) for i in range(k)]
     for c in copies:
         c.start()
@@ -466,7 +466,6 @@
         T, F = gate.shape
         H = R // 2
         W = 256
-        early = C
         out = lambda *s: jax.ShapeDtypeStruct(s, BF16)
         vmem_spec = pl.BlockSpec(memory_space=pltpu.VMEM)
         any_spec = pl.BlockSpec(memory_space=pl.ANY)
@@ -474,20 +473,8 @@
         vmem = lambda s, t: pltpu.VMEM(s, t)
         keep = lambda a: pltpu.with_memory_space_constraint(a, pltpu.VMEM)
 
-        def write(arrays, marks, name):
-            k = len(arrays)
-            return pl.pallas_call(
-                functools.partial(write_out, k),
-                out_shape=[out(*a.shape) for a in arrays] + [vmem((8, 128), F32)] * marks,
-                in_specs=[vmem_spec] * k,
-                out_specs=[any_spec] * k + [vmem_spec] * marks,
-                scratch_shapes=[dma((k,))],
-                compiler_params=pltpu.CompilerParams(vmem_limit_bytes=2**18),
-                name=name,
-            )(*(keep(a) for a in arrays))
-
         *dw, acc, last, _, _, _ = pl.pallas_call(
-            functools.partial(kernel, n, early),
+            functools.partial(kernel, n),
             out_shape=[vmem(s, BF16) for s in ((D, F), (D, F), (F, D))]
             + [vmem((R, D), F32), vmem((2, H, D), BF16), out(T, D), out(T, D), out(4, R, D)],
             in_specs=[any_spec] * 7,
@@ -512,9 +499,17 @@
             compiler_params=pltpu.CompilerParams(collective_id=0, has_side_effects=True, vmem_limit_bytes=199 * 2**18),
             name="mlp_backward",
         )(x, dy, gate, up, w_gate, w_up, w_down)
-        *dw, written = write(dw, 1, "write_weight_gradients")
+        *dw, written = pl.pallas_call(
+            write_out,
+            out_shape=[out(*a.shape) for a in dw] + [vmem((8, 128), F32)],
+            in_specs=[vmem_spec] * len(dw),
+            out_specs=[any_spec] * len(dw) + [vmem_spec],
+            scratch_shapes=[dma((len(dw),))],
+            compiler_params=pltpu.CompilerParams(vmem_limit_bytes=2**18),
+            name="write_weight_gradients",
+        )(*(keep(a) for a in dw))
         dx = pl.pallas_call(
-            functools.partial(last_hop, n, early),
+            functools.partial(last_hop, n),
             out_shape=vmem((R, D), BF16),
             in_specs=[vmem_spec] * 3,
             out_specs=vmem_spec,
@@ -522,7 +517,7 @@
             compiler_params=pltpu.CompilerParams(collective_id=1, has_side_effects=True, vmem_limit_bytes=2**22),
             name="last_hop",
         )(keep(acc), keep(last), keep(written))
-        return (write([dx], 0, "write_dx")[0], *dw)
+        return (dx, *dw)
 
     tok, col, row = P(("dp", "tp"), None), P("dp", "tp"), P("tp", None)
     wcol = P(None, "tp")

time: 210 us -> 210 us (level)
    pallas_call x4 -> x3, Pallas kernels: 209 us -> 208 us  [the longest x1 187 us: body(): pl.pallas_call(functools.partial(kernel, n), out_shape=[vmem(s, BF16) for...]
where the time goes in v5:
time: 210 us
  Pallas kernels  208 us (99%)
    pallas_call x1, Pallas kernels, body(): pl.pallas_call(functools.partial(kernel, n), out_shape=[vmem(s, BF16) for...  187 us
    pallas_call x1, Pallas kernels, body(): pl.pallas_call(functools.partial(last_hop, n), out_shape=vmem((R, D), BF1...  17.3 us

profile of v5, /device:TPU:112, one launch (start us, length us, event | category | flops | bytes accessed | tf_op | source)
XLA Modules:
  0.0 209.8 jit_solution(15183760280488400660)
XLA Ops:
  0.6 187.2 %mlp_backward.1 = (bf16[2048,640]{1,0:T(8,128)(2,1)S(1)}, bf16[2048,640]{1,0:T(8,128)(2,1)S(1)}, bf16[640,2048]{1,0:T(8,128)(2,1)S(1)}, f32[512,2048]{1,0:T(8,12...) custom-call(bf16[512,2048]{1,0:T(8,128)(2,1)} %x_ref.1, ...), custom_call_target="tpu_custom_call" | custom-call | tf_op jit(solution)/shard_map/mlp_backward/pallas_call | solution.py:476
  187.9 3.2 %write_weight_gradients.1 = (bf16[2048,640]{1,0:T(8,128)(2,1)}, bf16[2048,640]{1,0:T(8,128)(2,1)}, bf16[640,2048]{1,0:T(8,128)(2,1)}, f32[8,128]{1,0:T(8,128)S(1)}) custom-call(bf16[2048,640]{1,0:T(8,128)(2,1)S(1)} %get-tuple-element.15.refs_0_, bf16[2048,640]{1,0:T(8,128)(2,1)S(1)} %get-tuple-element.16.refs_1_, bf16[640,2048]{1,0:T(8,128)(2,1)S(1)} %get-tuple-element.17.refs_2_), custom_call_target="tpu_custom_call" | custom-call | tf_op jit(solution)/shard_map/write_weight_gradients/pallas_call | solution.py:502
  191.1 17.3 %last_hop.1 = bf16[512,2048]{1,0:T(8,128)(2,1)S(1)} custom-call(f32[512,2048]{1,0:T(8,128)S(1)} %get-tuple-element.13.acc_v, bf16[2,256,2048]{2,1,0:T(8,128)(2,1)S(1)} %get-tuple-element.14.last_v, f32[8,128]{1,0:T(8,128)S(1)} %get-tuple-element.18.after_ref), custom_call_target="tpu_custom_call" | custom-call | tf_op jit(solution)/shard_map/last_hop/pallas_call | solution.py:511
  208.5 1.3 copy.12

commit v6 on v5

--- a/solution.py
+++ b/solution.py
@@ -225,7 +225,8 @@
             psend[i % 2, :, cols] = v.astype(BF16)
 
         dx_terms(pl.multiple_of((block + other) * R, R), R, emit)
-        p_copy(i).start()
+        if i >= 1:
+            p_copy(i - 1).start()
 
     for k in (0, 2):
         ring_arrived(1, k)
@@ -233,6 +234,7 @@
         ring_fwd(1, k).start()
     for k in (0, 2):
         pair_fwd(1, k).start()
+    p_copy(3).start()
 
     def p_load(i, half=None):
         if half is None:
@@ -267,8 +269,8 @@
             dst[:, cols] = v.astype(BF16)
 
         dx_terms(pl.multiple_of(targets[i] * R + half * H, H), H, emit)
-        if q < 4:
-            q_part(q).start()
+        if 1 <= q < 4:
+            q_part(q - 1).start()
 
     p_fetch(0)
     p_fetch(1)
@@ -287,6 +289,7 @@
         acc_v[:, cols] = v + tile_v[1, :, cols].astype(F32)
 
     dx_terms(pl.multiple_of(me * R, R), R, emit_own)
+    q_part(3).start()
 
     for k in (1, 3):
         ring_arrived(1, k)
@@ -297,7 +300,7 @@
     def strip_load(a, t, slot):
         return local(full[a].at[:, pl.ds(pl.multiple_of(t * W, W), W)], strip_v.at[slot], st_sem.at[slot])
 
-    def strips(a, lo, hi, work):
+    def strips(a, lo, hi, work, after_first=lambda: None):
         strip_load(a, lo, lo % 2).start()
 
         def one(t, _):
@@ -309,6 +312,7 @@
                 strip_load(a, t + 1, 1 - slot).start()
 
             work(slot, pl.ds(pl.multiple_of(t * W, W), W))
+            pl.when(t == lo)(after_first)
             return 0
 
         lax.fori_loop(lo, hi, one, 0)
@@ -344,14 +348,14 @@
     ring_sum(4, 1, 0, add=0)
     ring_sum(5, 2, 1, add=1)
 
-    @pl.when(core == 1)
-    def _():
-        for sub in range(C):
-            for q in (4, 5):
-                q_part(q, sub).start()
-
-
-    strips(1, S // 2, S, in_work)
+    def send_last():
+        @pl.when(core == 1)
+        def _():
+            for sub in range(C):
+                for q in (4, 5):
+                    q_part(q, sub).start()
+
+    strips(1, S // 2, S, in_work, send_last)
 
     for a in range(2):
         for k in range(4):

time: 210 us -> 210 us (level)
  no operation moved by 1% of the time
where the time goes in v6:
time: 210 us
  Pallas kernels  208 us (99%)
    pallas_call x1, Pallas kernels, body(): pl.pallas_call(functools.partial(kernel, n), out_shape=[vmem(s, BF16) for...  187 us
    pallas_call x1, Pallas kernels, body(): pl.pallas_call(functools.partial(last_hop, n), out_shape=vmem((R, D), BF1...  17.3 us

profile of v6, /device:TPU:112, one launch (start us, length us, event | category | flops | bytes accessed | tf_op | source)
XLA Modules:
  0.0 209.8 jit_solution(14275088397641741706)
XLA Ops:
  0.6 187.2 %mlp_backward.1 = (bf16[2048,640]{1,0:T(8,128)(2,1)S(1)}, bf16[2048,640]{1,0:T(8,128)(2,1)S(1)}, bf16[640,2048]{1,0:T(8,128)(2,1)S(1)}, f32[512,2048]{1,0:T(8,12...) custom-call(bf16[512,2048]{1,0:T(8,128)(2,1)} %x_ref.1, ...), custom_call_target="tpu_custom_call" | custom-call | tf_op jit(solution)/shard_map/mlp_backward/pallas_call | solution.py:480
  187.9 3.2 %write_weight_gradients.1 = (bf16[2048,640]{1,0:T(8,128)(2,1)}, bf16[2048,640]{1,0:T(8,128)(2,1)}, bf16[640,2048]{1,0:T(8,128)(2,1)}, f32[8,128]{1,0:T(8,128)S(1)}) custom-call(bf16[2048,640]{1,0:T(8,128)(2,1)S(1)} %get-tuple-element.15.refs_0_, bf16[2048,640]{1,0:T(8,128)(2,1)S(1)} %get-tuple-element.16.refs_1_, bf16[640,2048]{1,0:T(8,128)(2,1)S(1)} %get-tuple-element.17.refs_2_), custom_call_target="tpu_custom_call" | custom-call | tf_op jit(solution)/shard_map/write_weight_gradients/pallas_call | solution.py:506
  191.1 17.3 %last_hop.1 = bf16[512,2048]{1,0:T(8,128)(2,1)S(1)} custom-call(f32[512,2048]{1,0:T(8,128)S(1)} %get-tuple-element.13.acc_v, bf16[2,256,2048]{2,1,0:T(8,128)(2,1)S(1)} %get-tuple-element.14.last_v, f32[8,128]{1,0:T(8,128)S(1)} %get-tuple-element.18.after_ref), custom_call_target="tpu_custom_call" | custom-call | tf_op jit(solution)/shard_map/last_hop/pallas_call | solution.py:515
  208.5 1.3 copy.12

commit v7 on v6

--- a/solution.py
+++ b/solution.py
@@ -122,11 +122,7 @@
         c.start()
     w_copies[1].start()
     w_copies[2].start()
-    for c in stage:
-        c.wait()
-    stage = [local(psend.at[0], dyg.at[rows(me)], own_sem.at[0]), local(psend.at[1], xg.at[rows(me)], own_sem.at[1])]
-    for c in stage:
-        c.start()
+    keep_own = [local(psend.at[0], dyg.at[rows(me)], own_sem.at[0]), local(psend.at[1], xg.at[rows(me)], own_sem.at[1])]
     w_copies[0].wait()
 
     def step(s, _):
@@ -139,6 +135,10 @@
 
         @pl.when(s == 0)
         def _():
+            for c in stage:
+                c.wait()
+            for c in keep_own:
+                c.start()
             pair_arrived(0, -1)
 
         @pl.when(s == 1)
@@ -197,10 +197,15 @@
         return 0
 
     lax.fori_loop(0, n, step, 0)
-    for c in stage:
+    for c in keep_own:
         c.wait()
     for c in w_copies[1:]:
         c.wait()
+
+    W = strip_v.shape[2]
+
+    def strip_load(a, t, slot):
+        return local(full[a].at[:, pl.ds(pl.multiple_of(t * W, W), W)], strip_v.at[slot], st_sem.at[slot])
 
     NB = 512
 
@@ -288,6 +293,7 @@
     def emit_own(cols, v):
         acc_v[:, cols] = v + tile_v[1, :, cols].astype(F32)
 
+    strip_load(0, 0, 0).start()
     dx_terms(pl.multiple_of(me * R, R), R, emit_own)
     q_part(3).start()
 
@@ -295,14 +301,7 @@
         ring_arrived(1, k)
         pair_fwd(1, k).start()
 
-    W = strip_v.shape[2]
-
-    def strip_load(a, t, slot):
-        return local(full[a].at[:, pl.ds(pl.multiple_of(t * W, W), W)], strip_v.at[slot], st_sem.at[slot])
-
     def strips(a, lo, hi, work, after_first=lambda: None):
-        strip_load(a, lo, lo % 2).start()
-
         def one(t, _):
             slot = lax.rem(t, 2)
             strip_load(a, t, slot).wait()
@@ -335,10 +334,12 @@
     for k in (-1, 0, 1, 2, 3, 4, 5):
         pair_arrived(1, k)
 
-    strips(1, 0, S // 2, in_work)
-
+    strip_load(1, 0, 0).start()
     for i, half in ((1, 0), (2, 1)):
         p_load(i, half).start()
+    strips(1, 0, S // 2, in_work)
+
+    strip_load(1, S // 2, S // 2 % 2).start()
     for c in q_parts(0) + q_parts(1):
         c.wait_recv()
     for i, half in ((1, 0), (2, 1)):

time: 210 us -> 210 us (level)
  no operation moved by 1% of the time
where the time goes in v7:
time: 210 us
  Pallas kernels  208 us (99%)
    pallas_call x1, Pallas kernels, body(): pl.pallas_call(functools.partial(kernel, n), out_shape=[vmem(s, BF16) for...  187 us
    pallas_call x1, Pallas kernels, body(): pl.pallas_call(functools.partial(last_hop, n), out_shape=vmem((R, D), BF1...  17.3 us

profile of v7, /device:TPU:112, one launch (start us, length us, event | category | flops | bytes accessed | tf_op | source)
XLA Modules:
  0.0 209.8 jit_solution(4646693407532571054)
XLA Ops:
  0.6 187.2 %mlp_backward.1 = (bf16[2048,640]{1,0:T(8,128)(2,1)S(1)}, bf16[2048,640]{1,0:T(8,128)(2,1)S(1)}, bf16[640,2048]{1,0:T(8,128)(2,1)S(1)}, f32[512,2048]{1,0:T(8,12...) custom-call(bf16[512,2048]{1,0:T(8,128)(2,1)} %x_ref.1, ...), custom_call_target="tpu_custom_call" | custom-call | tf_op jit(solution)/shard_map/mlp_backward/pallas_call | solution.py:481
  187.9 3.2 %write_weight_gradients.1 = (bf16[2048,640]{1,0:T(8,128)(2,1)}, bf16[2048,640]{1,0:T(8,128)(2,1)}, bf16[640,2048]{1,0:T(8,128)(2,1)}, f32[8,128]{1,0:T(8,128)S(1)}) custom-call(bf16[2048,640]{1,0:T(8,128)(2,1)S(1)} %get-tuple-element.15.refs_0_, bf16[2048,640]{1,0:T(8,128)(2,1)S(1)} %get-tuple-element.16.refs_1_, bf16[640,2048]{1,0:T(8,128)(2,1)S(1)} %get-tuple-element.17.refs_2_), custom_call_target="tpu_custom_call" | custom-call | tf_op jit(solution)/shard_map/write_weight_gradients/pallas_call | solution.py:507
  191.1 17.3 %last_hop.1 = bf16[512,2048]{1,0:T(8,128)(2,1)S(1)} custom-call(f32[512,2048]{1,0:T(8,128)S(1)} %get-tuple-element.13.acc_v, bf16[2,256,2048]{2,1,0:T(8,128)(2,1)S(1)} %get-tuple-element.14.last_v, f32[8,128]{1,0:T(8,128)S(1)} %get-tuple-element.18.after_ref), custom_call_target="tpu_custom_call" | custom-call | tf_op jit(solution)/shard_map/last_hop/pallas_call | solution.py:516
  208.5 1.3 copy.12

commit v8 on v7

--- a/solution.py
+++ b/solution.py
@@ -22,7 +22,7 @@
     n, x_ref, dy_ref, gate_ref, up_ref, wg_ref, wu_ref, wd_ref,
     dwg_ref, dwu_ref, dwd_ref, acc_v, last_v, dyg, xg, pbuf,
     wgu_v, dgu_v, hid_v, tile_v, gu_v, dh_v, psend, rsend, rrecv, strip_v,
-    ag_s, ag_r, p_s, p_r, q_s, q_r, w_sem, g_sem, t_sem, own_sem, st_sem,
+    side_sem, ag_s, ag_r, p_s, p_r, q_s, q_r, w_sem, g_sem, t_sem, own_sem, st_sem,
 ):
     me = lax.axis_index("tp")
     core = lax.rem(me, 2)
@@ -89,12 +89,26 @@
     )
 
     barrier = pltpu.get_barrier_semaphore()
-    for to in (left, right, partner):
+    for to in (left, right):
         pl.semaphore_signal(barrier, inc=1, device_id={"tp": to}, device_id_type=MESH)
-    pl.semaphore_wait(barrier, 3)
+
+    @pl.when(core == 1)
+    def _():
+        pl.semaphore_signal(barrier, inc=1, device_id={"tp": partner}, device_id_type=MESH)
+
+    pl.semaphore_wait(barrier, 3 - core)
+
+    @pl.when(core == 0)
+    def _():
+        pl.semaphore_signal(side_sem, inc=1, device_id={"tp": partner}, device_id_type=MESH)
 
     for k in (0, 2, 1, 3):
         ring_own(0, k).start()
+
+    @pl.when(core == 1)
+    def _():
+        pl.semaphore_wait(side_sem, 1)
+
     pair_own(0).start()
     pair_own(1).start()
 
@@ -495,6 +509,7 @@
                 pltpu.VMEM((4, H, D), BF16),
                 pltpu.VMEM((6, H, D), BF16),
                 pltpu.VMEM((2, T, W), BF16),
+                pltpu.SemaphoreType.REGULAR,
                 dma((2, 13)), dma((2, 13)),
                 dma((4,)), dma((4,)),
                 dma((4 + 2 * C,)), dma((4 + 2 * C,)),

time: 210 us -> 210 us (level)
  no operation moved by 1% of the time
where the time goes in v8:
time: 210 us
  Pallas kernels  208 us (99%)
    pallas_call x1, Pallas kernels, body(): pl.pallas_call(functools.partial(kernel, n), out_shape=[vmem(s, BF16) for...  187 us
    pallas_call x1, Pallas kernels, body(): pl.pallas_call(functools.partial(last_hop, n), out_shape=vmem((R, D), BF1...  17.1 us

profile of v8, /device:TPU:112, one launch (start us, length us, event | category | flops | bytes accessed | tf_op | source)
XLA Modules:
  0.0 209.6 jit_solution(4213399861378457968)
XLA Ops:
  0.6 187.3 %mlp_backward.1 = (bf16[2048,640]{1,0:T(8,128)(2,1)S(1)}, bf16[2048,640]{1,0:T(8,128)(2,1)S(1)}, bf16[640,2048]{1,0:T(8,128)(2,1)S(1)}, f32[512,2048]{1,0:T(8,12...) custom-call(bf16[512,2048]{1,0:T(8,128)(2,1)} %x_ref.1, ...), custom_call_target="tpu_custom_call" | custom-call | tf_op jit(solution)/shard_map/mlp_backward/pallas_call | solution.py:495
  187.9 3.2 %write_weight_gradients.1 = (bf16[2048,640]{1,0:T(8,128)(2,1)}, bf16[2048,640]{1,0:T(8,128)(2,1)}, bf16[640,2048]{1,0:T(8,128)(2,1)}, f32[8,128]{1,0:T(8,128)S(1)}) custom-call(bf16[2048,640]{1,0:T(8,128)(2,1)S(1)} %get-tuple-element.15.refs_0_, bf16[2048,640]{1,0:T(8,128)(2,1)S(1)} %get-tuple-element.16.refs_1_, bf16[640,2048]{1,0:T(8,128)(2,1)S(1)} %get-tuple-element.17.refs_2_), custom_call_target="tpu_custom_call" | custom-call | tf_op jit(solution)/shard_map/write_weight_gradients/pallas_call | solution.py:522
  191.1 17.1 %last_hop.1 = bf16[512,2048]{1,0:T(8,128)(2,1)S(1)} custom-call(f32[512,2048]{1,0:T(8,128)S(1)} %get-tuple-element.13.acc_v, bf16[2,256,2048]{2,1,0:T(8,128)(2,1)S(1)} %get-tuple-element.14.last_v, f32[8,128]{1,0:T(8,128)S(1)} %get-tuple-element.18.after_ref), custom_call_target="tpu_custom_call" | custom-call | tf_op jit(solution)/shard_map/last_hop/pallas_call | solution.py:531
  208.3 1.3 copy.12

commit v9 on v8

--- a/solution.py
+++ b/solution.py
@@ -247,6 +247,45 @@
         if i >= 1:
             p_copy(i - 1).start()
 
+    def p_load(i, half=None):
+        if half is None:
+            return local(pbuf.at[i], tile_v.at[i % 2], t_sem.at[i % 2])
+        h = pl.ds(half * H, H)
+        return local(pbuf.at[i, h], tile_v.at[i % 2, h], t_sem.at[i % 2])
+
+    def p_fetch(i):
+        p_copy(i).wait_recv()
+        p_load(i).start()
+
+    PIECE = H // C
+
+    def q_src(q):
+        return rsend.at[q] if q < 4 else last_v.at[q - 4]
+
+    def q_part(q, sub=None):
+        h, k = (pl.ds(0, H), q) if sub is None else (pl.ds(pl.multiple_of(sub * PIECE, PIECE), PIECE), q + 2 * sub)
+        return remote(q_src(q).at[h], rrecv.at[q, h], q_s.at[k], q_r.at[k], (right, left)[q % 2])
+
+    def q_parts(q):
+        return [q_part(q)] if q < 4 else [q_part(q, sub) for sub in range(C)]
+
+    def ring_sum(q, i, half, add=None):
+        h = pl.ds(half * H, H)
+        dst = q_src(q)
+
+        def emit(cols, v):
+            v = v + tile_v[i % 2, h, cols].astype(F32)
+            if add is not None:
+                v = v + rrecv[add, :, cols].astype(F32)
+            dst[:, cols] = v.astype(BF16)
+
+        dx_terms(pl.multiple_of(targets[i] * R + half * H, H), H, emit)
+        if 1 <= q < 4:
+            q_part(q - 1).start()
+
+    p_fetch(0)
+    p_fetch(1)
+
     for k in (0, 2):
         ring_arrived(1, k)
     for k in (4, 5):
@@ -255,44 +294,6 @@
         pair_fwd(1, k).start()
     p_copy(3).start()
 
-    def p_load(i, half=None):
-        if half is None:
-            return local(pbuf.at[i], tile_v.at[i % 2], t_sem.at[i % 2])
-        h = pl.ds(half * H, H)
-        return local(pbuf.at[i, h], tile_v.at[i % 2, h], t_sem.at[i % 2])
-
-    def p_fetch(i):
-        p_copy(i).wait_recv()
-        p_load(i).start()
-
-    PIECE = H // C
-
-    def q_src(q):
-        return rsend.at[q] if q < 4 else last_v.at[q - 4]
-
-    def q_part(q, sub=None):
-        h, k = (pl.ds(0, H), q) if sub is None else (pl.ds(pl.multiple_of(sub * PIECE, PIECE), PIECE), q + 2 * sub)
-        return remote(q_src(q).at[h], rrecv.at[q, h], q_s.at[k], q_r.at[k], (right, left)[q % 2])
-
-    def q_parts(q):
-        return [q_part(q)] if q < 4 else [q_part(q, sub) for sub in range(C)]
-
-    def ring_sum(q, i, half, add=None):
-        h = pl.ds(half * H, H)
-        dst = q_src(q)
-
-        def emit(cols, v):
-            v = v + tile_v[i % 2, h, cols].astype(F32)
-            if add is not None:
-                v = v + rrecv[add, :, cols].astype(F32)
-            dst[:, cols] = v.astype(BF16)
-
-        dx_terms(pl.multiple_of(targets[i] * R + half * H, H), H, emit)
-        if 1 <= q < 4:
-            q_part(q - 1).start()
-
-    p_fetch(0)
-    p_fetch(1)
     p_load(0).wait()
     ring_sum(0, 0, 0)
     ring_sum(1, 0, 1)
@@ -315,7 +316,7 @@
         ring_arrived(1, k)
         pair_fwd(1, k).start()
 
-    def strips(a, lo, hi, work, after_first=lambda: None):
+    def strips(a, lo, hi, work, after_first=lambda: None, before_last=lambda: None):
         def one(t, _):
             slot = lax.rem(t, 2)
             strip_load(a, t, slot).wait()
@@ -324,6 +325,7 @@
             def _():
                 strip_load(a, t + 1, 1 - slot).start()
 
+            pl.when(t + 1 == hi)(before_last)
             work(slot, pl.ds(pl.multiple_of(t * W, W), W))
             pl.when(t == lo)(after_first)
             return 0
@@ -340,15 +342,16 @@
         dwu_ref[part] = v[:, F:].astype(BF16)
 
     S = D // W
-    strips(0, 0, S, down_work)
-
-    for k in (4, 5):
-        ring_arrived(1, k)
-        pair_fwd(1, k).start()
-    for k in (-1, 0, 1, 2, 3, 4, 5):
-        pair_arrived(1, k)
-
-    strip_load(1, 0, 0).start()
+    def x_complete():
+        for k in (4, 5):
+            ring_arrived(1, k)
+            pair_fwd(1, k).start()
+        for k in (-1, 0, 1, 2, 3, 4, 5):
+            pair_arrived(1, k)
+        strip_load(1, 0, 0).start()
+
+    strips(0, 0, S, down_work, before_last=x_complete)
+
     for i, half in ((1, 0), (2, 1)):
         p_load(i, half).start()
     strips(1, 0, S // 2, in_work)

time: 210 us -> 210 us (level)
  no operation moved by 1% of the time
where the time goes in v9:
time: 210 us
  Pallas kernels  208 us (99%)
    pallas_call x1, Pallas kernels, body(): pl.pallas_call(functools.partial(kernel, n), out_shape=[vmem(s, BF16) for...  187 us
    pallas_call x1, Pallas kernels, body(): pl.pallas_call(functools.partial(last_hop, n), out_shape=vmem((R, D), BF1...  17.1 us

profile of v9, /device:TPU:112, one launch (start us, length us, event | category | flops | bytes accessed | tf_op | source)
XLA Modules:
  0.0 209.6 jit_solution(124394474320648964)
XLA Ops:
  0.6 187.3 %mlp_backward.1 = (bf16[2048,640]{1,0:T(8,128)(2,1)S(1)}, bf16[2048,640]{1,0:T(8,128)(2,1)S(1)}, bf16[640,2048]{1,0:T(8,128)(2,1)S(1)}, f32[512,2048]{1,0:T(8,12...) custom-call(bf16[512,2048]{1,0:T(8,128)(2,1)} %x_ref.1, ...), custom_call_target="tpu_custom_call" | custom-call | tf_op jit(solution)/shard_map/mlp_backward/pallas_call | solution.py:498
  187.9 3.2 %write_weight_gradients.1 = (bf16[2048,640]{1,0:T(8,128)(2,1)}, bf16[2048,640]{1,0:T(8,128)(2,1)}, bf16[640,2048]{1,0:T(8,128)(2,1)}, f32[8,128]{1,0:T(8,128)S(1)}) custom-call(bf16[2048,640]{1,0:T(8,128)(2,1)S(1)} %get-tuple-element.15.refs_0_, bf16[2048,640]{1,0:T(8,128)(2,1)S(1)} %get-tuple-element.16.refs_1_, bf16[640,2048]{1,0:T(8,128)(2,1)S(1)} %get-tuple-element.17.refs_2_), custom_call_target="tpu_custom_call" | custom-call | tf_op jit(solution)/shard_map/write_weight_gradients/pallas_call | solution.py:525
  191.1 17.1 %last_hop.1 = bf16[512,2048]{1,0:T(8,128)(2,1)S(1)} custom-call(f32[512,2048]{1,0:T(8,128)S(1)} %get-tuple-element.13.acc_v, bf16[2,256,2048]{2,1,0:T(8,128)(2,1)S(1)} %get-tuple-element.14.last_v, f32[8,128]{1,0:T(8,128)S(1)} %get-tuple-element.18.after_ref), custom_call_target="tpu_custom_call" | custom-call | tf_op jit(solution)/shard_map/last_hop/pallas_call | solution.py:534
  208.3 1.3 copy.12

commit v10 on v8

--- a/solution.py
+++ b/solution.py
@@ -433,8 +433,8 @@
             device_id={"tp": to[q]}, device_id_type=MESH,
         )
 
-    def finish(lo, count, add):
-        for q in range(2):
+    def finish(lo, count, add, halves=(0, 1)):
+        for q in halves:
             def put(i, _):
                 h = pl.ds(pl.multiple_of(lo + i * 16, 16), 16)
                 r = pl.ds(pl.multiple_of(q * H + lo + i * 16, 16), 16)
@@ -454,10 +454,10 @@
 
         def each(sub, _):
             for q in range(2):
+                part(q, sub).wait_send()
+            for q in range(2):
                 part(q, sub).wait_recv()
-            finish(sub * PIECE, PIECE, True)
-            for q in range(2):
-                part(q, sub).wait_send()
+                finish(sub * PIECE, PIECE, True, (q,))
             return 0
 
         lax.fori_loop(0, C, each, 0)

time: 210 us -> 210 us (level)
  no operation moved by 1% of the time
where the time goes in v10:
time: 210 us
  Pallas kernels  208 us (99%)
    pallas_call x1, Pallas kernels, body(): pl.pallas_call(functools.partial(kernel, n), out_shape=[vmem(s, BF16) for...  187 us
    pallas_call x1, Pallas kernels, body(): pl.pallas_call(functools.partial(last_hop, n), out_shape=vmem((R, D), BF1...  17.1 us

profile of v10, /device:TPU:112, one launch (start us, length us, event | category | flops | bytes accessed | tf_op | source)
XLA Modules:
  0.0 209.6 jit_solution(13726607548789795123)
XLA Ops:
  0.6 187.3 %mlp_backward.1 = (bf16[2048,640]{1,0:T(8,128)(2,1)S(1)}, bf16[2048,640]{1,0:T(8,128)(2,1)S(1)}, bf16[640,2048]{1,0:T(8,128)(2,1)S(1)}, f32[512,2048]{1,0:T(8,12...) custom-call(bf16[512,2048]{1,0:T(8,128)(2,1)} %x_ref.1, ...), custom_call_target="tpu_custom_call" | custom-call | tf_op jit(solution)/shard_map/mlp_backward/pallas_call | solution.py:495
  187.9 3.2 %write_weight_gradients.1 = (bf16[2048,640]{1,0:T(8,128)(2,1)}, bf16[2048,640]{1,0:T(8,128)(2,1)}, bf16[640,2048]{1,0:T(8,128)(2,1)}, f32[8,128]{1,0:T(8,128)S(1)}) custom-call(bf16[2048,640]{1,0:T(8,128)(2,1)S(1)} %get-tuple-element.15.refs_0_, bf16[2048,640]{1,0:T(8,128)(2,1)S(1)} %get-tuple-element.16.refs_1_, bf16[640,2048]{1,0:T(8,128)(2,1)S(1)} %get-tuple-element.17.refs_2_), custom_call_target="tpu_custom_call" | custom-call | tf_op jit(solution)/shard_map/write_weight_gradients/pallas_call | solution.py:522
  191.1 17.1 %last_hop.1 = bf16[512,2048]{1,0:T(8,128)(2,1)S(1)} custom-call(f32[512,2048]{1,0:T(8,128)S(1)} %get-tuple-element.13.acc_v, bf16[2,256,2048]{2,1,0:T(8,128)(2,1)S(1)} %get-tuple-element.14.last_v, f32[8,128]{1,0:T(8,128)S(1)} %get-tuple-element.18.after_ref), custom_call_target="tpu_custom_call" | custom-call | tf_op jit(solution)/shard_map/last_hop/pallas_call | solution.py:531
  208.3 1.3 copy.12
